TPU v7x, 32 devices: a whole 2x2x4 slice. The times are simulated.
32 devices in a mesh: tm: 4 (over y, x), sky: 8 (over z, core).
Axes of the slice: x: 2, y: 2, z: 4, core: 2. Of those that a mesh axis runs over, the one named last changes fastest.
Arguments:
- residual: float32 [16384, 128], P(('tm', 'sky')), may hold values from -110 to 110
- obs_weight: float32 [16384, 128], P(('tm', 'sky')), may hold values from 0.5 to 2
- source_partials: float32 [5, 16384, 128], P(None, ('tm', 'sky')), may hold values from -1 to 1
- attitude_partials: float32 [16, 16384, 128], P(None, ('tm', 'sky')), may hold values from -1.5 to 1.5
- source_index: int32 [16384, 128], P(('tm', 'sky')), may hold values from 0 to 127
- tile_pixel: int32 [16384], P(('tm', 'sky')), may hold values from 0 to 1023, as said below
- tile_knot: int32 [16384], P(('tm', 'sky')), may hold values from 0 to 2047, as said below
- pixel_slot: int32 [1024], replicated, may hold values from 0 to 1023, as said below
Outputs:
- final_residual: float32 [16384, 128], P(('tm', 'sky'))
- source_update: float32 [5, 131072], P(None, 'sky')
- attitude_update: float32 [4, 2048], P(None, 'tm')
Inputs may be any that keep to these rules, and one draw needn't show every extreme that they name: Tiles come in aligned blocks of 512; with owner = pixel_slot[tile_pixel[t]] // 128, no block holds more than 192 tiles of one owner, and every block holds exactly 192 tiles of some owner. `pixel_slot`: every slot number appears once. `tile_knot`: the tiles of aligned block q of 512 tiles have first knots in [q * 64, (q + 1) * 64).
All inputs are finite; a program needn't handle non-finite values.
Results may differ from a plain program's by a relative error of at most 0.0003.
Values sent between devices are 32-bit elements; how exact they have to be, the bound alone decides.
A program may use at most 128 MiB of HBM per device.

v0:
```python
import functools

import jax
import jax.numpy as jnp
from jax import lax
from jax.experimental import pallas as pl
from jax.experimental.pallas import tpu as pltpu
from jax.sharding import PartitionSpec as P

PIX_DEV = 128
SRC_PIX = 128
KNOTS_DEV = 512


SOURCE_PAIRS = tuple(((first, second) for first in range(5) for second in range(first, 5)))
KNOT_PAIRS = tuple(((first, second) for first in range(4) for second in range(first, 4)))


def passed_along(value, axes, steps):
    count = 1
    for axis in axes:
        count *= lax.axis_size(axis)
    first, last = (max(0, -steps), min(count, count - steps))
    return lax.ppermute(value, axes, [(source, source + steps) for source in range(first, last)])


def damped_solve(normal, target, order, pairs):
    entries = {}
    for number, couple in enumerate(pairs):
        entries[couple] = normal[number]
    factor = {}
    for column in range(order):
        pivot_value = entries[column, column] + 1.0
        for earlier in range(column):
            pivot_value = pivot_value - factor[column, earlier] * factor[column, earlier]
        pivot_value = jnp.sqrt(pivot_value)
        factor[column, column] = pivot_value
        for below in range(column + 1, order):
            current = entries[column, below]
            for earlier in range(column):
                current = current - factor[below, earlier] * factor[column, earlier]
            factor[below, column] = current / pivot_value
    forward = []
    for column in range(order):
        current = target[column]
        for earlier in range(column):
            current = current - factor[column, earlier] * forward[earlier]
        forward.append(current / factor[column, column])
    answer = [None] * order
    for column in reversed(range(order)):
        current = forward[column]
        for later in range(column + 1, order):
            current = current - factor[later, column] * answer[later]
        answer[column] = current / factor[column, column]
    return jnp.stack(answer)


ROWS = 20
PAD = 24


def sums_kernel(pixel_ref, slot_ref, resid, weight, parts, index, out, acc, stage):
    tiles = resid.shape[0]
    chunks, _, run, _ = out.shape
    pixels = chunks * run

    def clear(step, carry):
        acc[pl.ds(pl.multiple_of(step * 192, 192), 192), :] = jnp.zeros((192, SRC_PIX), jnp.float32)
        return carry

    lax.fori_loop(0, pixels * PAD // 192, clear, 0)
    stage[...] = jnp.zeros_like(stage)
    sources = lax.broadcasted_iota(jnp.int32, (SRC_PIX, SRC_PIX), 0)

    def group(step, carry):
        base = pl.multiple_of(step * 8, 8)
        here = pl.ds(base, 8)
        fields = [parts[c, here, :] for c in range(5)]
        scaled = [weight[here, :] * field for field in fields]
        baseline = resid[here, :]
        row = 0
        for first, second in SOURCE_PAIRS:
            stage[pl.ds(row, 8, stride=PAD), :] = scaled[first] * fields[second]
            row += 1
        for first in range(5):
            stage[pl.ds(row, 8, stride=PAD), :] = scaled[first] * baseline
            row += 1
        ids = index[here, :]
        for j in range(8):
            seat = slot_ref[pixel_ref[base + j]]
            values = stage[j * PAD : (j + 1) * PAD, :]
            high = values.astype(jnp.bfloat16)
            low = (values - high.astype(jnp.float32)).astype(jnp.bfloat16)
            hits = jnp.where(sources == ids[j : j + 1, :], 1.0, 0.0).astype(jnp.bfloat16)
            both = lax.dot_general(
                jnp.concatenate([high, low], axis=0),
                hits,
                (((1,), (1,)), ((), ())),
                preferred_element_type=jnp.float32,
            )
            spot = pl.ds(pl.multiple_of(seat * PAD, 8), PAD)
            acc[spot, :] += both[:PAD] + both[PAD:]
        return carry

    lax.fori_loop(0, tiles // 8, group, 0)

    def unload(chunk, carry):
        for row in range(ROWS):
            for part in range(run // 8):
                start = (chunk * run + part * 8) * PAD + row
                out[chunk, row, part * 8 : part * 8 + 8, :] = acc[pl.ds(start, 8, stride=PAD), :]
        return carry

    lax.fori_loop(0, chunks, unload, 0)


def local_sums(tile_pixel, pixel_slot, residual, obs_weight, source_partials, source_index, chunks):
    pixels = pixel_slot.shape[0]
    return pl.pallas_call(
        sums_kernel,
        name="local_sums",
        out_shape=jax.ShapeDtypeStruct((chunks, ROWS, pixels // chunks, SRC_PIX), jnp.float32),
        in_specs=[pl.BlockSpec(memory_space=pltpu.SMEM)] * 2
        + [pl.BlockSpec(memory_space=pltpu.VMEM)] * 4,
        out_specs=pl.BlockSpec(memory_space=pltpu.VMEM),
        scratch_shapes=[
            pltpu.VMEM((pixels * PAD, SRC_PIX), jnp.float32),
            pltpu.VMEM((8 * PAD, SRC_PIX), jnp.float32),
        ],
        compiler_params=pltpu.CompilerParams(vmem_limit_bytes=60 * 1024 * 1024),
    )(tile_pixel, pixel_slot, residual, obs_weight, source_partials, source_index)


def settle_kernel(run, pixel_ref, slot_ref, resid, parts, index, table, out, rows):
    tiles = resid.shape[0]

    def group(step, carry):
        base = pl.multiple_of(step * 8, 8)
        here = pl.ds(base, 8)
        for j in range(8):
            seat = slot_ref[pixel_ref[base + j]]
            start = (seat // run) * (5 * run) + seat % run
            for c in range(5):
                rows[c, pl.ds(base + j, 1), :] = table[pl.ds(start + c * run, 1), :]
        ids = index[here, :]
        total = None
        for c in range(5):
            picked = jnp.take_along_axis(rows[c, here, :], ids, axis=1)
            addend = parts[c, here, :] * picked
            total = addend if total is None else total + addend
        out[here, :] = resid[here, :] - total
        return carry

    lax.fori_loop(0, tiles // 8, group, 0)


def settle(tile_pixel, pixel_slot, residual, source_partials, source_index, table, run):
    tiles = residual.shape[0]
    return pl.pallas_call(
        functools.partial(settle_kernel, run),
        name="settle",
        out_shape=jax.ShapeDtypeStruct(residual.shape, jnp.float32),
        in_specs=[pl.BlockSpec(memory_space=pltpu.SMEM)] * 2
        + [pl.BlockSpec(memory_space=pltpu.VMEM)] * 4,
        out_specs=pl.BlockSpec(memory_space=pltpu.VMEM),
        scratch_shapes=[pltpu.VMEM((5, tiles, SRC_PIX), jnp.float32)],
        compiler_params=pltpu.CompilerParams(vmem_limit_bytes=48 * 1024 * 1024),
    )(tile_pixel, pixel_slot, residual, source_partials, source_index, table)


def tile_rows(weights, partials, baseline, couples):
    rows = []
    for segment in range(4):
        portion = partials[4 * segment : 4 * segment + 4]
        for first, second in couples:
            other = baseline if second is None else portion[second]
            rows.append(jnp.sum(weights * portion[first] * other, axis=-1))
    return jnp.stack(rows)


def on_knots(rows, knot_hits, span):
    placed = jnp.dot(rows, knot_hits, precision=lax.Precision.HIGHEST)
    count = rows.shape[0] // 4
    total = jnp.zeros((count, span + 3), jnp.float32)
    for segment in range(4):
        part = placed[count * segment : count * (segment + 1)]
        total = total + jnp.pad(part, ((0, 0), (segment, 3 - segment)))
    return total


def body(
    residual,
    obs_weight,
    source_partials,
    attitude_partials,
    source_index,
    tile_pixel,
    tile_knot,
    pixel_slot,
):
    owners = lax.axis_size("sky")
    times = lax.axis_size("tm")
    chunks = owners * times
    run = PIX_DEV // times
    span = KNOTS_DEV // owners
    block = lax.axis_index("tm") * owners + lax.axis_index("sky")

    sums = local_sums(
        tile_pixel, pixel_slot, residual, obs_weight, source_partials, source_index, chunks
    )
    summed, late_weight = lax.optimization_barrier((reduce_chunks(sums), obs_weight))

    knot_start = tile_knot - block * span
    knot_hits = (knot_start[:, None] == jnp.arange(span, dtype=jnp.int32)[None, :]).astype(
        jnp.float32
    )
    square_rows = tile_rows(late_weight, attitude_partials, None, KNOT_PAIRS)
    squares = on_knots(square_rows, knot_hits, span)

    update = damped_solve(summed[:15], summed[15:], 5, SOURCE_PAIRS)
    table = gather_chunks(update)
    settled = settle(
        tile_pixel,
        pixel_slot,
        residual,
        source_partials,
        source_index,
        table.reshape(chunks * 5 * run, SRC_PIX),
        run,
    )
    mine = lax.dynamic_slice_in_dim(table, lax.axis_index("sky") * times, times, 0)
    source_update = mine.transpose(1, 0, 2, 3).reshape(5, PIX_DEV * SRC_PIX)

    target_rows = tile_rows(
        obs_weight, attitude_partials, settled, [(first, None) for first in range(4)]
    )
    targets = on_knots(target_rows, knot_hits, span)
    accumulated = jnp.concatenate([squares, targets], axis=0)
    axes = ("tm", "sky")
    arriving = passed_along(accumulated[:, span:], axes, 1)
    whole = accumulated[:, :span] + jnp.pad(arriving, ((0, 0), (0, span - 3)))
    own_update = damped_solve(whole[:10], whole[10:], 4, KNOT_PAIRS)
    following = passed_along(own_update[:, :3], axes, -1)
    extended = jnp.concatenate([own_update, following], axis=1)
    attitude_update = lax.all_gather(own_update, "sky", axis=1, tiled=True)
    windows = jnp.concatenate([extended[:, seg : seg + span] for seg in range(4)], axis=0)
    values = jnp.dot(windows, knot_hits.T, precision=lax.Precision.HIGHEST)
    total = None
    for number in range(16):
        addend = attitude_partials[number] * values[number][:, None]
        total = addend if total is None else total + addend
    return (settled - total, source_update, attitude_update)


def add_rows(count, target, *sources):
    def one(row, carry):
        total = sources[0][row]
        for source in sources[1:]:
            total = total + source[row]
        target[row] = total
        return carry

    lax.fori_loop(0, count, one, 0)


def reduce_kernel(times, lines, sums, out, got0, got1, part, got2, *sems):
    send0, recv0, send1, recv1, send2, recv2 = sems
    mesh_ids = pl.DeviceIdType.MESH
    time, sky = lax.axis_index("tm"), lax.axis_index("sky")
    line, core = sky // 2, sky % 2
    time_peers = [lax.rem(time + step, times) for step in range(1, times)]
    line_peers = [lax.rem(line + step, lines) for step in range(1, lines)]
    partner = (time, sky + 1 - 2 * core)

    barrier = pltpu.get_barrier_semaphore()
    peers = [partner] + [(peer, sky) for peer in time_peers]
    peers += [(time, peer * 2 + core) for peer in line_peers]
    for peer in peers:
        pl.semaphore_signal(barrier, inc=1, device_id=peer, device_id_type=mesh_ids)
    pl.semaphore_wait(barrier, len(peers))

    pieces = line_peers + [line]
    first = []
    for step, piece in enumerate(pieces):
        copy = pltpu.make_async_remote_copy(
            src_ref=sums.at[piece, 1 - core],
            dst_ref=got0.at[step],
            send_sem=send0.at[step],
            recv_sem=recv0.at[step],
            device_id=partner,
            device_id_type=mesh_ids,
        )
        copy.start()
        first.append(copy)
    second = []
    for step, piece in enumerate(pieces):
        first[step].wait_recv()
        for slot in range(times):
            target = got0.at[step, slot]
            add_rows(ROWS, target, target, sums.at[piece, core, slot])
        copies = []
        for number, peer in enumerate(time_peers):
            copy = pltpu.make_async_remote_copy(
                src_ref=got0.at[step, peer],
                dst_ref=got1.at[step, number],
                send_sem=send1.at[step, number],
                recv_sem=recv1.at[step, number],
                device_id=(peer, sky),
                device_id_type=mesh_ids,
            )
            copy.start()
            copies.append(copy)
        second.append(copies)
    third = []
    for step, piece in enumerate(pieces):
        for copy in second[step]:
            copy.wait_recv()
        arrived = [got1.at[step, number] for number in range(times - 1)]
        add_rows(ROWS, part.at[step], got0.at[step, time], *arrived)
        if step < lines - 1:
            copy = pltpu.make_async_remote_copy(
                src_ref=part.at[step],
                dst_ref=got2.at[step],
                send_sem=send2.at[step],
                recv_sem=recv2.at[step],
                device_id=(time, piece * 2 + core),
                device_id_type=mesh_ids,
            )
            copy.start()
            third.append(copy)
    for copy in third:
        copy.wait_recv()
    arrived = [got2.at[step] for step in range(lines - 1)]
    add_rows(ROWS, out, part.at[lines - 1], *arrived)
    for copy in first + [copy for copies in second for copy in copies] + third:
        copy.wait_send()


def reduce_chunks(sums):
    times, owners = lax.axis_size("tm"), lax.axis_size("sky")
    lines = owners // 2
    unit = sums.shape[1:]
    dma = pltpu.SemaphoreType.DMA
    return pl.pallas_call(
        functools.partial(reduce_kernel, times, lines),
        name="reduce_chunks",
        out_shape=jax.ShapeDtypeStruct(unit, jnp.float32),
        in_specs=[pl.BlockSpec(memory_space=pltpu.VMEM)],
        out_specs=pl.BlockSpec(memory_space=pltpu.VMEM),
        scratch_shapes=[
            pltpu.VMEM((lines, times) + unit, jnp.float32),
            pltpu.VMEM((lines, times - 1) + unit, jnp.float32),
            pltpu.VMEM((lines,) + unit, jnp.float32),
            pltpu.VMEM((lines - 1,) + unit, jnp.float32),
            dma((lines,)),
            dma((lines,)),
            dma((lines, times - 1)),
            dma((lines, times - 1)),
            dma((lines - 1,)),
            dma((lines - 1,)),
        ],
        compiler_params=pltpu.CompilerParams(
            collective_id=0, has_side_effects=True, vmem_limit_bytes=62 * 1024 * 1024
        ),
    )(sums.reshape((lines, 2, times) + unit))


def gather_kernel(times, lines, update, table, send0, recv0, send1, recv1, send2, recv2):
    mesh_ids = pl.DeviceIdType.MESH
    time, sky = lax.axis_index("tm"), lax.axis_index("sky")
    line, core = sky // 2, sky % 2
    time_peers = [lax.rem(time + step, times) for step in range(1, times)]
    line_peers = [lax.rem(line + step, lines) for step in range(1, lines)]
    partner = (time, sky + 1 - 2 * core)

    barrier = pltpu.get_barrier_semaphore()
    peers = [partner] + [(peer, sky) for peer in time_peers]
    peers += [(time, peer * 2 + core) for peer in line_peers]
    for peer in peers:
        pl.semaphore_signal(barrier, inc=1, device_id=peer, device_id_type=mesh_ids)
    pl.semaphore_wait(barrier, len(peers))

    def send(source, target, send_sem, recv_sem, peer):
        copy = pltpu.make_async_remote_copy(
            src_ref=source,
            dst_ref=target,
            send_sem=send_sem,
            recv_sem=recv_sem,
            device_id=peer,
            device_id_type=mesh_ids,
        )
        copy.start()
        return copy

    own = table.at[sky * times + time]
    first = []
    for number, peer in enumerate(line_peers):
        spot = (time, peer * 2 + core)
        first.append(send(update, own, send0.at[number], recv0.at[number], spot))
    own[...] = update[...]
    sources = [line] + [lax.rem(line + lines - step, lines) for step in range(1, lines)]
    second = []
    for step, source in enumerate(sources):
        place = table.at[(source * 2 + core) * times + time]
        if step > 0:
            first[step - 1].wait_recv()
        held = place if step > 0 else update
        second.append(
            [
                send(held, place, send1.at[step, number], recv1.at[step, number], (peer, sky))
                for number, peer in enumerate(time_peers)
            ]
        )
    third = []
    for step, source in enumerate(sources):
        for copy in second[step]:
            copy.wait_recv()
        place = table.at[pl.ds((source * 2 + core) * times, times)]
        third.append(send(place, place, send2.at[step], recv2.at[step], partner))
    for copy in third:
        copy.wait_recv()
    for copy in first + [copy for copies in second for copy in copies] + third:
        copy.wait_send()


def gather_chunks(update):
    times, owners = lax.axis_size("tm"), lax.axis_size("sky")
    lines = owners // 2
    dma = pltpu.SemaphoreType.DMA
    return pl.pallas_call(
        functools.partial(gather_kernel, times, lines),
        name="gather_chunks",
        out_shape=jax.ShapeDtypeStruct((owners * times,) + update.shape, jnp.float32),
        in_specs=[pl.BlockSpec(memory_space=pltpu.VMEM)],
        out_specs=pl.BlockSpec(memory_space=pltpu.VMEM),
        scratch_shapes=[
            dma((lines - 1,)),
            dma((lines - 1,)),
            dma((lines, times - 1)),
            dma((lines, times - 1)),
            dma((lines,)),
            dma((lines,)),
        ],
        compiler_params=pltpu.CompilerParams(
            collective_id=1, has_side_effects=True, vmem_limit_bytes=16 * 1024 * 1024
        ),
    )(update)


def solution(mesh):
    in_specs = (
        P(("tm", "sky"), None),
        P(("tm", "sky"), None),
        P(None, ("tm", "sky"), None),
        P(None, ("tm", "sky"), None),
        P(("tm", "sky"), None),
        P(("tm", "sky")),
        P(("tm", "sky")),
        P(),
    )
    out_specs = (P(("tm", "sky"), None), P(None, "sky"), P(None, "tm"))
    return jax.shard_map(body, mesh=mesh, in_specs=in_specs, out_specs=out_specs, check_vma=False)
```

profile of v0, /device:TPU:0, one launch (start us, length us, event | category | flops | bytes accessed | tf_op | source)
XLA Modules:
  0.0 165.2 jit_solution(16441820691305906666)
XLA Ops:
  0.6 27.7 %local_sums.1 = f32[32,20,32,128]{3,2,1,0:T(8,128)} custom-call(s32[512]{0:T(512)} %pixel_ref.3, s32[1024]{0:T(1024)} %slot_ref.3, f32[512,128]{1,0:T(8,128)} %resid.3, f32[512,128]{1,0:T(8,128)} %weight.1, f32[5,512,128]{2,1,0:T(8,128)} %parts.3, s32[512,128]{1,0:T(8,128)} %index.3), custom_call_target="tpu_custom_call" | custom-call | tf_op jit(solution)/shard_map/local_sums/pallas_call | solution.py:119
  28.4 72.2 %reduce_chunks.1 = f32[20,32,128]{2,1,0:T(8,128)} custom-call(f32[4,2,4,20,32,128]{5,4,3,2,1,0:T(8,128)} %bitcast.431), custom_call_target="tpu_custom_call" | custom-call | tf_op jit(solution)/shard_map/reduce_chunks/pallas_call | solution.py:344
  100.6 3.3 %bitcast_multiply_fusion.59 = (f32[512,128]{1,0:T(8,128)S(1)}, f32[512,128]{1,0:T(8,128)S(1)}, f32[512,128]{1,0:T(8,128)S(1)}, f32[512]{0:T(512)S(1)}, f32[512]{...) fusion(f32[512,128]{1,0:T(8,128)S(1)} %copy-done.7, ...), kind=kLoop, calls=%fused_computation.129 | loop fusion | flops 2810880 | bytes 5533696 | tf_op jit(solution)/shard_map/mul | solution.py:177
  103.9 0.1 copy-done.5
  104.0 1.1 fusion.3
  105.2 2.8 %fusion.4 = (f32[512]{0:T(512)S(1)}, f32[512]{0:T(512)S(1)}, f32[512]{0:T(512)S(1)}, f32[512]{0:T(512)S(1)}, f32[512]{0:T(512)S(1)}, /*index=5*/f32[512]{0:T(512...) fusion(f32[512,128]{1,0:T(8,128)S(1)} %get-tuple-element.102, ...), kind=kLoop, calls=%fused_computation.15 | loop fusion | flops 1566720 | bytes 3956736 | tf_op jit(solution)/shard_map/reduce_sum | solution.py:177
  107.9 0.2 stack.230
  108.1 0.3 fusion.90
  108.6 0.1 divide_dynamic-update-slice_fusion
  108.7 20.1 %gather_chunks.1 = f32[32,5,32,128]{3,2,1,0:T(8,128)S(1)} custom-call(f32[5,32,128]{2,1,0:T(8,128)S(1)} %constant_dynamic-update-slice_fusion.update), custom_call_target="tpu_custom_call" | custom-call | tf_op jit(solution)/shard_map/gather_chunks/pallas_call | solution.py:430
  128.9 1.3 copy-done
  130.2 8.5 %settle.1 = f32[512,128]{1,0:T(8,128)S(1)} custom-call(s32[512]{0:T(512)S(1)} %copy-done.4, s32[1024]{0:T(1024)S(1)} %copy-done.3, f32[512,128]{1,0:T(8,128)S(1)} %copy-done.1, f32[5,512,128]{2,1,0:T(8,128)S(1)} %copy-done, s32[512,128]{1,0:T(8,128)S(1)} %copy-done.2, f32[5120,128]{1,0:T(8,128)S(1)} %bitcast.430), custom_call_target="tpu_custom_call" | custom-call | tf_op jit(solution)/shard_map/settle/pallas_call | solution.py:159
  138.7 1.2 fusion.10
  139.8 0.1 stack.247
  139.9 0.3 fusion.89
  140.2 0.1 pad_add_fusion
  140.4 0.1 pad_maximum_fusion
  140.5 2.3 %collective-permute-start = (f32[14,3]{1,0:T(8,128)S(1)}, f32[14,3]{1,0:T(8,128)S(1)}, u32[]{:S(2)}, u32[]{:S(2)}) collective-permute-start(f32[14,3]{1,0:T(8,128)S(1)} %pad_maximum_fusion), channel_id=1, source_target_pairs={{0,1},{1,2},{2,3},{3,4},{4,5},{5,6},{6,7},{7,8},{8,9},{9,10},{10,1... | collective-permute-start | bytes 512 | tf_op jit(solution)/shard_map/ppermute | solution.py:24
  142.8 1.0 copy.17
  144.0 1.3 collective-permute-start.1
  145.3 14.1 %all-gather = f32[8,64,4]{1,2,0:T(4,128)S(1)} all-gather(f32[1,64,4]{1,2,0:T(4,128)S(1)} %get-tuple-element.150), channel_id=1, replica_groups=mesh['tm'=4,'sky'=8] {'sky'}, dimensions={0}, use_global_device_ids=true | all-gather | bytes 9216 | tf_op jit(solution)/shard_map/all_gather | solution.py:245
  159.4 0.7 reshape.36
  160.2 0.3 fusion.88
  160.6 4.6 %fusion.8 = f32[512,128]{1,0:T(8,128)} fusion(f32[512,128]{1,0:T(8,128)S(1)} %settle.1, f32[16,512,128]{2,1,0:T(8,128)} %param.11, f32[512]{0:T(512)S(1)} %bitcast.475, f32[512]{0:T(512)S(1)} %bitcast.476, f32[512]{0:T(512)S(1)} %bitcast.477, f32[512]{0:T(512)S(1)} %bitcast.478, f32[512]{0:T(512)S(1)} %bitcast.479, f32[512]{0:T(512)S(1)} %bitcast.480, ...), kind=kLoop, calls=%fused_computation.19 | loop fusion | flops 2097152 | bytes 4751360 | tf_op jit(solution)/shard_map/sub | solution.py:252
  (44 shorter events, 0.7 us)
Async XLA Ops:
  28.4 72.2 %copy-start.7 = (f32[512,128]{1,0:T(8,128)S(1)}, f32[512,128]{1,0:T(8,128)}, u32[]{:S(2)}) copy-start(f32[512,128]{1,0:T(8,128)} %weight.1) | copy-start | bytes 786436
  100.6 3.4 %copy-start.5 = (f32[16,512,128]{2,1,0:T(8,128)S(1)}, f32[16,512,128]{2,1,0:T(8,128)}, u32[]{:S(2)}) copy-start(f32[16,512,128]{2,1,0:T(8,128)} %param.11) | copy-start | bytes 12582916
  100.6 4.6 %copy-start.10 = (s32[512]{0:T(512)S(1)}, s32[512]{0:T(512)}, u32[]{:S(2)}) copy-start(s32[512]{0:T(512)} %param.14) | copy-start | bytes 6148
  104.0 4.4 %copy-start.9 = (f32[20,32,128]{2,1,0:T(8,128)S(1)}, f32[20,32,128]{2,1,0:T(8,128)}, u32[]{:S(2)}) copy-start(f32[20,32,128]{2,1,0:T(8,128)} %reduce_chunks.1) | copy-start | bytes 983044
  105.1 23.7 %copy-start.1 = (f32[512,128]{1,0:T(8,128)S(1)}, f32[512,128]{1,0:T(8,128)}, u32[]{:S(2)}) copy-start(f32[512,128]{1,0:T(8,128)} %resid.3) | copy-start | bytes 786436
  105.1 23.7 %copy-start.2 = (s32[512,128]{1,0:T(8,128)S(1)}, s32[512,128]{1,0:T(8,128)}, u32[]{:S(2)}) copy-start(s32[512,128]{1,0:T(8,128)} %index.3) | copy-start | bytes 786436
  105.1 23.7 %copy-start.3 = (s32[1024]{0:T(1024)S(1)}, s32[1024]{0:T(1024)}, u32[]{:S(2)}) copy-start(s32[1024]{0:T(1024)} %slot_ref.3) | copy-start | bytes 12292
  105.1 23.7 %copy-start.4 = (s32[512]{0:T(512)S(1)}, s32[512]{0:T(512)}, u32[]{:S(2)}) copy-start(s32[512]{0:T(512)} %pixel_ref.3) | copy-start | bytes 6148
  108.5 30.1 %copy-start.8 = (f32[512,128]{1,0:T(8,128)S(1)}, f32[512,128]{1,0:T(8,128)}, u32[]{:S(2)}) copy-start(f32[512,128]{1,0:T(8,128)} %weight.1) | copy-start | bytes 786436
  128.9 1.3 copy-start
  130.2 8.5 %copy-start.6 = (f32[16,512,128]{2,1,0:T(8,128)S(1)}, f32[16,512,128]{2,1,0:T(8,128)}, u32[]{:S(2)}) copy-start(f32[16,512,128]{2,1,0:T(8,128)} %param.11) | copy-start | bytes 12582916
  140.5 3.4 %collective-permute-start = (f32[14,3]{1,0:T(8,128)S(1)}, f32[14,3]{1,0:T(8,128)S(1)}, u32[]{:S(2)}, u32[]{:S(2)}) collective-permute-start(f32[14,3]{1,0:T(8,128)S(1)} %pad_maximum_fusion), channel_id=1, source_target_pairs={{0,1},{1,2},{2,3},{3,4},{4,5},{5,6},{6,7},{7,8},{8,9},{9,10},{10,1... | collective-permute-start | bytes 512 | tf_op jit(solution)/shard_map/ppermute | solution.py:24
  144.0 16.1 %collective-permute-start.1 = (f32[4,3]{1,0:T(4,128)S(1)}, f32[4,3]{1,0:T(4,128)S(1)}, u32[]{:S(2)}, u32[]{:S(2)}) collective-permute-start(f32[4,3]{1,0:T(4,128)S(1)} %bitcast.507), channel_id=1, source_target_pairs={{1,0},{2,1},{3,2},{4,3},{5,4},{6,5},{7,6},{8,7},{9,8},{10,9},{11,1... | collective-permute-start | bytes 152 | tf_op jit(solution)/shard_map/ppermute | solution.py:24
where the time goes:
time: 168 us; the launch traced here: 165 us
  Pallas kernels  128 us (76%)
  blocking collectives  14.1 us (8%)
  other arithmetic  13.6 us (8%)
  local copies, waits for them, and re-layouts  3.64 us (2%)
  starting transfers between devices  3.59 us (2%)
    pallas_call x1, Pallas kernels, reduce_chunks(): pl.pallas_call(functools.partial(reduce_kernel, times, lines), name='redu...  72.2 us
    pallas_call x1, Pallas kernels, local_sums(): pl.pallas_call(sums_kernel, name='local_sums', out_shape=jax.ShapeDtypeSt...  27.7 us
    pallas_call x1, Pallas kernels, gather_chunks(): pl.pallas_call(functools.partial(gather_kernel, times, lines), name='gath...  20.1 us
    all_gather x1, blocking collectives, body(): attitude_update = lax.all_gather(own_update, 'sky', axis=1, tiled=True)  14.1 us
    pallas_call x1, Pallas kernels, settle(): pl.pallas_call(functools.partial(settle_kernel, run), name='settle', out_...  8.46 us
    reduce_sum x3, other arithmetic, tile_rows(): rows.append(jnp.sum(weights * portion[first] * other, axis=-1))  5.03 us
    sub x1, other arithmetic, body(): return (settled - total, source_update, attitude_update)  4.58 us
    ppermute x2, starting transfers between devices, passed_along(): lax.ppermute(value, axes, [(source, source + steps) for source in range(f...  3.59 us
  transfers between devices with their start and end apart: 2, of which 0 were waited for; matrix products, arithmetic and copies ran while one was open for 1% of the time, Pallas kernels for 0%

commit v1 on v0

v1 whole, which is shorter than its diff:
```python
import functools

import jax
import jax.numpy as jnp
from jax import lax
from jax.experimental import pallas as pl
from jax.experimental.pallas import tpu as pltpu
from jax.sharding import PartitionSpec as P

KNOTS_DEV = 512
ROWS = 20
PAD = 24
UPD = 5
LANES = 128
SUB = 8
MIB = 1024 * 1024

SOURCE_PAIRS = tuple(((first, second) for first in range(5) for second in range(first, 5)))
KNOT_PAIRS = tuple(((first, second) for first in range(4) for second in range(first, 4)))


def damped_solve(normal, target, order, pairs):
    entries = {}
    for number, couple in enumerate(pairs):
        entries[couple] = normal[number]
    factor = {}
    for column in range(order):
        pivot_value = entries[column, column] + 1.0
        for earlier in range(column):
            pivot_value = pivot_value - factor[column, earlier] * factor[column, earlier]
        pivot_value = jnp.sqrt(pivot_value)
        factor[column, column] = pivot_value
        for below in range(column + 1, order):
            current = entries[column, below]
            for earlier in range(column):
                current = current - factor[below, earlier] * factor[column, earlier]
            factor[below, column] = current / pivot_value
    forward = []
    for column in range(order):
        current = target[column]
        for earlier in range(column):
            current = current - factor[column, earlier] * forward[earlier]
        forward.append(current / factor[column, column])
    answer = [None] * order
    for column in reversed(range(order)):
        current = forward[column]
        for later in range(column + 1, order):
            current = current - factor[later, column] * answer[later]
        answer[column] = current / factor[column, column]
    return answer


def split_times(times):
    inner = 2 if times % 2 == 0 else 1
    return times // inner, inner


def sums_kernel(times, owners, tiles_step, pixel_ref, slot_ref, resid, weight, parts, index, out, stage, prods):
    tiles = resid.shape[0]
    outer, inner = split_times(times)
    pixels = out.shape[0] // ROWS
    per_owner = pixels // owners
    run = per_owner // times
    half = run // 2
    zero = jnp.zeros((256, LANES), jnp.float32)

    def clear(step, carry):
        out[pl.ds(pl.multiple_of(step * 256, 256), 256), :] = zero
        return carry

    lax.fori_loop(0, pixels * ROWS // 256, clear, 0)
    stage[...] = jnp.zeros_like(stage)
    prods[...] = jnp.zeros_like(prods)
    sources = lax.broadcasted_iota(jnp.int32, (SUB, LANES), 0).astype(jnp.float32)
    bands = [
        jnp.concatenate([sources + float(16 * band), sources + float(16 * band + 8)], axis=0).astype(jnp.bfloat16)
        for band in range(LANES // 16)
    ]
    lanes_of = jnp.concatenate(bands, axis=0)
    one = jnp.ones((LANES, LANES), jnp.bfloat16)
    none = jnp.zeros((LANES, LANES), jnp.bfloat16)

    def place(tile):
        seat = slot_ref[pixel_ref[tile]]
        owner, rest = seat // per_owner, seat % per_owner
        time, spot = rest // run, rest % run
        low_half = spot // half
        time_out, time_in = time // inner, time % inner
        order = jnp.where(low_half == 0, time_in * outer + time_out, time)
        return (((owner * 2 + low_half) * times + order) * half + spot % half) * ROWS

    def accumulate(step, slot):
        for j in range(tiles_step):
            start = place(step * tiles_step + j)
            values = prods[pl.ds(slot * tiles_step * PAD + j * PAD, PAD), :]
            out[pl.ds(start, ROWS), :] += values[:ROWS]

    def multiply(step, slot):
        for part in range(tiles_step // SUB):
            base = pl.multiple_of(step * tiles_step + part * SUB, SUB)
            here = pl.ds(base, SUB)
            fields = [parts[c, here, :] for c in range(5)]
            scaled = [weight[here, :] * field for field in fields]
            baseline = resid[here, :]
            row = part * SUB * PAD
            for first, second in SOURCE_PAIRS:
                stage[pl.ds(row, SUB, stride=PAD), :] = scaled[first] * fields[second]
                row += 1
            for first in range(5):
                stage[pl.ds(row, SUB, stride=PAD), :] = scaled[first] * baseline
                row += 1
            ids = index[here, :].astype(jnp.float32)
            for j in range(SUB):
                number = part * SUB + j
                values = stage[number * PAD : (number + 1) * PAD, :]
                high = values.astype(jnp.bfloat16).astype(jnp.float32)
                both = jnp.concatenate([high, values - high], axis=0).astype(jnp.bfloat16)
                wide = jnp.broadcast_to(ids[j : j + 1, :], (16, LANES)).astype(jnp.bfloat16)
                hits = jnp.where(lanes_of == jnp.concatenate([wide] * (LANES // 16), axis=0), one, none)
                got = lax.dot_general(
                    both, hits, (((1,), (1,)), ((), ())), preferred_element_type=jnp.float32
                )
                prods[pl.ds(slot * tiles_step * PAD + number * PAD, PAD), :] = got[:PAD] + got[PAD:]

    steps = tiles // tiles_step
    multiply(0, 0)

    def pair(step, carry):
        multiply(2 * step + 1, 1)
        accumulate(2 * step, 0)
        multiply(jnp.minimum(2 * step + 2, steps - 1), 0)
        accumulate(2 * step + 1, 1)
        return carry

    lax.fori_loop(0, steps // 2, pair, 0)


def local_sums(tile_pixel, pixel_slot, residual, obs_weight, source_partials, source_index, times, owners):
    pixels = pixel_slot.shape[0]
    tiles_step = 16
    return pl.pallas_call(
        functools.partial(sums_kernel, times, owners, tiles_step),
        name="local_sums",
        out_shape=jax.ShapeDtypeStruct((pixels * ROWS, LANES), jnp.float32),
        in_specs=[pl.BlockSpec(memory_space=pltpu.SMEM)] * 2 + [pl.BlockSpec(memory_space=pltpu.VMEM)] * 4,
        out_specs=pl.BlockSpec(memory_space=pltpu.VMEM),
        scratch_shapes=[
            pltpu.VMEM((tiles_step * PAD, LANES), jnp.float32),
            pltpu.VMEM((2 * tiles_step * PAD, LANES), jnp.float32),
        ],
        compiler_params=pltpu.CompilerParams(vmem_limit_bytes=30 * MIB),
    )(tile_pixel, pixel_slot, residual, obs_weight, source_partials, source_index)


def add_rows(target, *sources):
    rows = target.shape[0]
    step_rows = 32
    while rows % step_rows:
        step_rows //= 2

    def one(step, carry):
        here = pl.ds(pl.multiple_of(step * step_rows, step_rows), step_rows)
        total = sources[0][here, :]
        for source in sources[1:]:
            total = total + source[here, :]
        target[here, :] = total
        return carry

    lax.fori_loop(0, rows // step_rows, one, 0)


def square_sums(weight, att, rows, first, last):
    lane = lax.broadcasted_iota(jnp.int32, (SUB, LANES), 1)

    def group(step, carry):
        here = pl.ds(pl.multiple_of(step * SUB, SUB), SUB)
        scale = weight[here, :]
        total = jnp.zeros((SUB, LANES), jnp.float32)
        for m in range(4):
            fields = [att[4 * m + c, here, :] for c in range(4)]
            scaled = [scale * field for field in fields]
            for number, (a, b) in enumerate(KNOT_PAIRS):
                value = jnp.sum(scaled[a] * fields[b], axis=1, keepdims=True)
                total = jnp.where(lane == 16 * m + number, value, total)
        rows[here, :] = total
        return carry

    lax.fori_loop(first, last, group, 0)


def exchange_kernel(
    times, lines, sums, weight, att, table, squares, got0, a1, b1, a2, b2, part, got2, upd, *sems
):
    s0, r0, sa1, ra1, sb1, rb1, sa2, ra2, sb2, rb2, s3, r3, su, ru, st, rt, sd, rd = sems
    outer, inner = split_times(times)
    mesh_ids = pl.DeviceIdType.MESH
    time, sky = lax.axis_index("tm"), lax.axis_index("sky")
    line, core = sky // 2, sky % 2
    mo, mi = time // inner, time % inner
    partner = (time, sky + 1 - 2 * core)
    half_rows = a2.shape[2]
    tiles = weight.shape[0]
    inner_at = [lax.rem(mi + step, inner) for step in range(1, inner)]
    outer_at = [lax.rem(mo + step, outer) for step in range(1, outer)]
    inner_peers = [(mo * inner + i, sky) for i in inner_at]
    outer_peers = [(o * inner + mi, sky) for o in outer_at]
    steps = sorted(range(1, lines), key=lambda step: -min(step, lines - step)) + [0]
    pieces = [lax.rem(line + step, lines) for step in steps]
    line_peers = [(time, piece * 2 + core) for piece in pieces[:-1]]

    barrier = pltpu.get_barrier_semaphore()
    peers = [partner] + inner_peers + outer_peers + line_peers
    for peer in peers:
        pl.semaphore_signal(barrier, inc=1, device_id=peer, device_id_type=mesh_ids)
    pl.semaphore_wait(barrier, len(peers))

    pending = []

    def send(source, target, send_sem, recv_sem, peer):
        copy = pltpu.make_async_remote_copy(
            src_ref=source, dst_ref=target, send_sem=send_sem, recv_sem=recv_sem,
            device_id=peer, device_id_type=mesh_ids,
        )
        copy.start()
        pending.append(copy)
        return copy

    count = len(pieces)
    zeroth = [
        send(sums.at[piece, 1 - core], got0.at[step], s0.at[step], r0.at[step], partner)
        for step, piece in enumerate(pieces)
    ]
    first_a, first_b, second_a, second_b, third = {}, {}, {}, {}, {}

    def stage_one(k):
        zeroth[k].wait_recv()
        for side in range(2):
            add_rows(got0.at[k, side], got0.at[k, side], sums.at[pieces[k], core, side])
            if side == 0:
                first_a[k] = [
                    send(
                        got0.at[k, 0, pl.ds(i * outer * half_rows, outer * half_rows)],
                        a1.at[k, number], sa1.at[k, number], ra1.at[k, number], peer,
                    )
                    for number, (i, peer) in enumerate(zip(inner_at, inner_peers))
                ]
            else:
                first_b[k] = [
                    send(
                        got0.at[k, 1, pl.ds(o * inner * half_rows, inner * half_rows)],
                        b1.at[k, number], sb1.at[k, number], rb1.at[k, number], peer,
                    )
                    for number, (o, peer) in enumerate(zip(outer_at, outer_peers))
                ]

    def stage_two(k):
        for copy in first_a[k]:
            copy.wait_recv()
        mine = got0.at[k, 0, pl.ds(mi * outer * half_rows, outer * half_rows)]
        if inner > 1:
            add_rows(mine, mine, *[a1.at[k, number] for number in range(inner - 1)])
        second_a[k] = [
            send(
                got0.at[k, 0, pl.ds((mi * outer + o) * half_rows, half_rows)],
                a2.at[k, number], sa2.at[k, number], ra2.at[k, number], peer,
            )
            for number, (o, peer) in enumerate(zip(outer_at, outer_peers))
        ]
        for copy in first_b[k]:
            copy.wait_recv()
        mine = got0.at[k, 1, pl.ds(mo * inner * half_rows, inner * half_rows)]
        if outer > 1:
            add_rows(mine, mine, *[b1.at[k, number] for number in range(outer - 1)])
        second_b[k] = [
            send(
                got0.at[k, 1, pl.ds((mo * inner + i) * half_rows, half_rows)],
                b2.at[k, number], sb2.at[k, number], rb2.at[k, number], peer,
            )
            for number, (i, peer) in enumerate(zip(inner_at, inner_peers))
        ]

    def stage_three(k):
        for copy in second_a[k]:
            copy.wait_recv()
        own = got0.at[k, 0, pl.ds((mi * outer + mo) * half_rows, half_rows)]
        add_rows(part.at[k, pl.ds(0, half_rows)], own, *[a2.at[k, number] for number in range(outer - 1)])
        for copy in second_b[k]:
            copy.wait_recv()
        own = got0.at[k, 1, pl.ds((mo * inner + mi) * half_rows, half_rows)]
        add_rows(
            part.at[k, pl.ds(half_rows, half_rows)], own, *[b2.at[k, number] for number in range(inner - 1)]
        )
        if k < count - 1:
            third[k] = send(part.at[k], got2.at[k], s3.at[k], r3.at[k], line_peers[k])

    groups = tiles // SUB
    stage_one(0)
    if count > 1:
        stage_one(1)
    square_sums(weight, att, squares, 0, groups // 2)
    for k in range(count):
        stage_two(k)
        if k + 2 < count:
            stage_one(k + 2)
        if k == 0:
            square_sums(weight, att, squares, groups // 2, groups)
        if k > 0:
            stage_three(k - 1)
    stage_three(count - 1)
    for k in range(count - 1):
        third[k].wait_recv()
    total = part.at[count - 1]
    add_rows(total, total, *[got2.at[k] for k in range(count - 1)])

    run = 2 * half_rows // ROWS
    block = run * UPD

    def solve(step, carry):
        base = step * SUB
        entry = [
            part[count - 1, pl.ds(base * ROWS + row, SUB, stride=ROWS), :] for row in range(ROWS)
        ]
        answer = damped_solve(entry[:15], entry[15:], 5, SOURCE_PAIRS)
        for c in range(UPD):
            upd[pl.ds(base * UPD + c, SUB, stride=UPD), :] = answer[c]
        return carry

    lax.fori_loop(0, run // SUB, solve, 0)

    half_block = block // 2

    def spot(source_line, source_core, source_time):
        return pl.multiple_of(((source_line * 2 + source_core) * times + source_time) * block, SUB)

    own = table.at[pl.ds(spot(line, core, time), block)]
    from_line = []
    for number, peer in enumerate(line_peers):
        from_line.append(send(upd, own, su.at[number], ru.at[number], peer))
    sources = [lax.rem(line + lines - step, lines) for step in steps[:-1]]
    order = [count - 1] + sorted(range(count - 1), key=lambda n: min(steps[n], lines - steps[n]))
    near, far = {}, {}

    def spread(n):
        source = line if n == count - 1 else sources[n]
        place = table.at[pl.ds(spot(source, core, time), block)]
        if n < count - 1:
            from_line[n].wait_recv()
            held = place
        else:
            held = upd
        near[n] = [
            send(held, place, st.at[n, number], rt.at[n, number], peer)
            for number, peer in enumerate(inner_peers + outer_peers)
        ]
        return source

    def relay(n, source):
        far[n] = []
        number = inner + outer - 2
        for which, copy in enumerate(near[n]):
            copy.wait_recv()
            from_inner = which < inner - 1
            if from_inner:
                origin = mo * inner + lax.rem(mi + inner - (which + 1), inner)
                rows, targets = 0, outer_peers
            else:
                origin = lax.rem(mo + outer - (which - inner + 2), outer) * inner + mi
                rows, targets = half_block, inner_peers
            piece = table.at[pl.ds(spot(source, core, origin) + rows, half_block)]
            for peer in targets:
                far[n].append(send(piece, piece, st.at[n, number], rt.at[n, number], peer))
                number += 1

    def finish(n, source):
        for copy in far[n]:
            copy.wait_recv()
        place = table.at[pl.ds(spot(source, core, 0), times * block)]
        return send(place, place, sd.at[n], rd.at[n], partner)

    held_rows = pl.multiple_of(spot(line, core, time), SUB)
    spread_sources = {order[0]: spread(order[0])}
    table[pl.ds(held_rows, block), :] = upd[...]
    last = []
    for at, n in enumerate(order):
        if at + 1 < count:
            spread_sources[order[at + 1]] = spread(order[at + 1])
        relay(n, spread_sources[n])
        if at > 0:
            last.append(finish(order[at - 1], spread_sources[order[at - 1]]))
    last.append(finish(order[-1], spread_sources[order[-1]]))
    for copy in last:
        copy.wait_recv()
    for copy in pending:
        copy.wait_send()


def exchange(sums, obs_weight, attitude_partials):
    times, owners = lax.axis_size("tm"), lax.axis_size("sky")
    lines = owners // 2
    outer, inner = split_times(times)
    total_rows = sums.shape[0]
    half_rows = total_rows // (owners * times * 2)
    pixels = total_rows // ROWS
    block = pixels // (owners * times) * UPD
    tiles = obs_weight.shape[0]
    dma = pltpu.SemaphoreType.DMA
    vmem = pltpu.VMEM
    near = inner + outer - 2
    far = 2 * (inner - 1) * (outer - 1)
    f32 = jnp.float32

    def pair(*shape):
        return [dma(shape), dma(shape)]

    return pl.pallas_call(
        functools.partial(exchange_kernel, times, lines),
        name="exchange",
        out_shape=(
            jax.ShapeDtypeStruct((pixels * UPD + SUB, LANES), f32),
            jax.ShapeDtypeStruct((tiles, LANES), f32),
        ),
        in_specs=[pl.BlockSpec(memory_space=pltpu.VMEM)] * 3,
        out_specs=(pl.BlockSpec(memory_space=pltpu.VMEM),) * 2,
        scratch_shapes=[
            vmem((lines, 2, times * half_rows, LANES), f32),
            vmem((lines, max(inner - 1, 1), outer * half_rows, LANES), f32),
            vmem((lines, max(outer - 1, 1), inner * half_rows, LANES), f32),
            vmem((lines, max(outer - 1, 1), half_rows, LANES), f32),
            vmem((lines, max(inner - 1, 1), half_rows, LANES), f32),
            vmem((lines, 2 * half_rows, LANES), f32),
            vmem((max(lines - 1, 1), 2 * half_rows, LANES), f32),
            vmem((block, LANES), f32),
        ]
        + pair(lines)
        + pair(lines, max(inner - 1, 1))
        + pair(lines, max(outer - 1, 1))
        + pair(lines, max(outer - 1, 1))
        + pair(lines, max(inner - 1, 1))
        + pair(lines)
        + pair(lines)
        + pair(lines, near + far)
        + pair(lines),
        compiler_params=pltpu.CompilerParams(
            collective_id=0, has_side_effects=True, vmem_limit_bytes=44 * MIB
        ),
    )(sums.reshape(lines, 2, 2, times * half_rows, LANES), obs_weight, attitude_partials)


def thirds(value):
    high = value.astype(jnp.bfloat16)
    rest = value - high.astype(jnp.float32)
    middle = rest.astype(jnp.bfloat16)
    return high, middle, (rest - middle.astype(jnp.float32)).astype(jnp.bfloat16)


def settle_kernel(pixel_ref, slot_ref, knots, resid, weight, parts, att, index, table, squares, out, sums, rows, terms):
    tiles = resid.shape[0]
    lane = lax.broadcasted_iota(jnp.int32, (SUB, LANES), 1)

    def group(step, carry):
        base = pl.multiple_of(step * SUB, SUB)
        here = pl.ds(base, SUB)
        for j in range(SUB):
            seat = slot_ref[pixel_ref[base + j]]
            rows[j * SUB : (j + 1) * SUB, :] = table[pl.ds(seat * UPD, SUB), :]
        ids = index[here, :]
        total = None
        for c in range(UPD):
            picked = jnp.take_along_axis(rows[pl.ds(c, SUB, stride=SUB), :], ids, axis=1)
            addend = parts[c, here, :] * picked
            total = addend if total is None else total + addend
        settled = resid[here, :] - total
        out[here, :] = settled
        scaled = weight[here, :] * settled
        term = squares[here, :]
        for m in range(4):
            for c in range(4):
                value = jnp.sum(scaled * att[4 * m + c, here, :], axis=1, keepdims=True)
                term = jnp.where(lane == 16 * m + 10 + c, value, term)
        terms[here, :] = term
        return carry

    lax.fori_loop(0, tiles // SUB, group, 0)
    knot = lax.broadcasted_iota(jnp.int32, (LANES, tiles), 0)
    hits = jnp.where(knot == knots[...], 1.0, 0.0).astype(jnp.bfloat16)
    placed = None
    for piece in thirds(terms[...]):
        got = jnp.dot(hits, piece, preferred_element_type=jnp.float32)
        placed = got if placed is None else placed + got
    turned = placed.T
    total = turned[:16]
    for m in range(1, 4):
        total = total + pltpu.roll(turned[16 * m : 16 * m + 16], m, 1)
    sums[...] = total


def settle(tile_pixel, pixel_slot, knots, residual, obs_weight, source_partials, attitude_partials, source_index, table, squares):
    tiles = residual.shape[0]
    return pl.pallas_call(
        settle_kernel,
        name="settle",
        out_shape=(
            jax.ShapeDtypeStruct(residual.shape, jnp.float32),
            jax.ShapeDtypeStruct((16, LANES), jnp.float32),
        ),
        in_specs=[pl.BlockSpec(memory_space=pltpu.SMEM)] * 2 + [pl.BlockSpec(memory_space=pltpu.VMEM)] * 8,
        out_specs=(pl.BlockSpec(memory_space=pltpu.VMEM),) * 2,
        scratch_shapes=[pltpu.VMEM((SUB * SUB, LANES), jnp.float32), pltpu.VMEM((tiles, LANES), jnp.float32)],
        compiler_params=pltpu.CompilerParams(vmem_limit_bytes=32 * MIB),
    )(tile_pixel, pixel_slot, knots, residual, obs_weight, source_partials, attitude_partials, source_index, table, squares)


def finish_kernel(
    times, owners, span, sums, knots, settled, att, table, out, source_out, knot_out,
    before, mine, others, after, values, sa, ra, sb, rb, sc, rc,
):
    mesh_ids = pl.DeviceIdType.MESH
    time, sky = lax.axis_index("tm"), lax.axis_index("sky")
    blocks = times * owners
    block = time * owners + sky
    nxt, prev = lax.rem(block + 1, blocks), lax.rem(block + blocks - 1, blocks)
    next_id, prev_id = (nxt // owners, lax.rem(nxt, owners)), (prev // owners, lax.rem(prev, owners))
    peers = [(time, lax.rem(sky + step, owners)) for step in range(1, owners)]

    barrier = pltpu.get_barrier_semaphore()
    for peer in [next_id, prev_id] + peers:
        pl.semaphore_signal(barrier, inc=1, device_id=peer, device_id_type=mesh_ids)
    pl.semaphore_wait(barrier, owners + 1)

    pending = []

    def send(source, target, send_sem, recv_sem, peer):
        copy = pltpu.make_async_remote_copy(
            src_ref=source, dst_ref=target, send_sem=send_sem, recv_sem=recv_sem,
            device_id=peer, device_id_type=mesh_ids,
        )
        copy.start()
        pending.append(copy)
        return copy

    handed = send(sums, before, sa, ra, next_id)

    per_owner = source_out.shape[1] // LANES

    def spread(pixel, carry):
        place = pl.ds(pl.multiple_of(pixel * LANES, LANES), LANES)
        source_out[:, place] = table[pl.ds((sky * per_owner + pixel) * UPD, UPD), :]
        return carry

    lax.fori_loop(0, per_owner, spread, 0)

    lane = lax.broadcasted_iota(jnp.int32, (16, LANES), 1)
    handed.wait_recv()
    arrived = pltpu.roll(before[...], LANES - span, 1)
    arrived = jnp.where((lane < 3) & (block > 0), arrived, 0.0)
    whole = jnp.where(lane < span, sums[...], 0.0) + arrived
    answer = damped_solve(
        [whole[n : n + 1] for n in range(10)], [whole[n : n + 1] for n in range(10, 14)], 4, KNOT_PAIRS
    )
    for c in range(4):
        mine[c : c + 1, :] = answer[c]
        mine[4 + c : 5 + c, :] = answer[c]
    back = send(mine, after, sb, rb, prev_id)
    around = [
        send(mine, others.at[sky], sc.at[number], rc.at[number], peer)
        for number, peer in enumerate(peers)
    ]
    back.wait_recv()
    lane = lax.broadcasted_iota(jnp.int32, (SUB, LANES), 1)
    following = jnp.where(block < blocks - 1, after[...], 0.0)
    extended = jnp.where(lane < span, mine[...], 0.0)
    extended = extended + jnp.where(
        (lane >= span) & (lane < span + 3), pltpu.roll(following, span, 1), 0.0
    )
    windows = []
    for m in range(0, 4, 2):
        low = extended if m == 0 else pltpu.roll(extended, LANES - m, 1)
        high = pltpu.roll(extended, LANES - m - 1, 1)
        half = lax.broadcasted_iota(jnp.int32, (SUB, LANES), 0) < 4
        windows.append(jnp.where(half, low, high))
    window = jnp.concatenate(windows, axis=0)
    tiles = settled.shape[0]
    knot = lax.broadcasted_iota(jnp.int32, (LANES, tiles), 0)
    hits = jnp.where(knot == knots[...], 1.0, 0.0).astype(jnp.bfloat16)
    picked = None
    for piece in thirds(window):
        got = jnp.dot(piece, hits, preferred_element_type=jnp.float32)
        picked = got if picked is None else picked + got
    for part in range(tiles // LANES):
        values[part * LANES : (part + 1) * LANES, :] = picked[:, part * LANES : (part + 1) * LANES].T

    def group(step, carry):
        here = pl.ds(pl.multiple_of(step * SUB, SUB), SUB)
        column = values[here, :]
        total = None
        for number in range(16):
            addend = att[number, here, :] * column[:, number : number + 1]
            total = addend if total is None else total + addend
        out[here, :] = settled[here, :] - total
        return carry

    lax.fori_loop(0, tiles // SUB, group, 0)
    for copy in around:
        copy.wait_recv()
    others[pl.ds(sky, 1)] = mine[...][None]
    each = LANES // span
    for first in range(0, owners, each):
        joined = jnp.where(lane < span, others[first], 0.0)
        for number in range(1, each):
            moved = pltpu.roll(others[first + number], number * span, 1)
            keep = (lane >= number * span) & (lane < (number + 1) * span)
            joined = jnp.where(keep, moved, joined)
        knot_out[:, first * span : first * span + LANES] = joined[:4]
    for copy in pending:
        copy.wait_send()


def finish(sums, knots, settled, attitude_partials, table, span):
    times, owners = lax.axis_size("tm"), lax.axis_size("sky")
    tiles = settled.shape[0]
    dma = pltpu.SemaphoreType.DMA
    f32 = jnp.float32
    pixels = (table.shape[0] - SUB) // UPD
    return pl.pallas_call(
        functools.partial(finish_kernel, times, owners, span),
        name="finish",
        out_shape=(
            jax.ShapeDtypeStruct(settled.shape, f32),
            jax.ShapeDtypeStruct((UPD, pixels // owners * LANES), f32),
            jax.ShapeDtypeStruct((4, span * owners), f32),
        ),
        in_specs=[pl.BlockSpec(memory_space=pltpu.VMEM)] * 5,
        out_specs=(pl.BlockSpec(memory_space=pltpu.VMEM),) * 3,
        scratch_shapes=[
            pltpu.VMEM((16, LANES), f32),
            pltpu.VMEM((SUB, LANES), f32),
            pltpu.VMEM((owners, SUB, LANES), f32),
            pltpu.VMEM((SUB, LANES), f32),
            pltpu.VMEM((tiles, 16), f32),
            dma, dma, dma, dma, dma((owners - 1,)), dma((owners - 1,)),
        ],
        compiler_params=pltpu.CompilerParams(
            collective_id=1, has_side_effects=True, vmem_limit_bytes=32 * MIB
        ),
    )(sums, knots, settled, attitude_partials, table)


def body(residual, obs_weight, source_partials, attitude_partials, source_index, tile_pixel, tile_knot, pixel_slot):
    owners = lax.axis_size("sky")
    times = lax.axis_size("tm")
    span = KNOTS_DEV // owners
    block = lax.axis_index("tm") * owners + lax.axis_index("sky")
    knots = (tile_knot - block * span)[None, :]
    sums = local_sums(
        tile_pixel, pixel_slot, residual, obs_weight, source_partials, source_index, times, owners
    )
    table, squares = exchange(sums, obs_weight, attitude_partials)
    settled, knot_sums = settle(
        tile_pixel, pixel_slot, knots, residual, obs_weight, source_partials, attitude_partials,
        source_index, table, squares,
    )
    return finish(knot_sums, knots, settled, attitude_partials, table, span)


def solution(mesh):
    in_specs = (
        P(("tm", "sky"), None),
        P(("tm", "sky"), None),
        P(None, ("tm", "sky"), None),
        P(None, ("tm", "sky"), None),
        P(("tm", "sky"), None),
        P(("tm", "sky")),
        P(("tm", "sky")),
        P(),
    )
    out_specs = (P(("tm", "sky"), None), P(None, "sky"), P(None, "tm"))
    return jax.shard_map(body, mesh=mesh, in_specs=in_specs, out_specs=out_specs, check_vma=False)
```

time: 168 us -> 147 us (0.88); the launches traced: 165 us -> 147 us
  blocking collectives: 14.1 us -> 0 us
  other arithmetic: 13.6 us -> 0.69 us
  local copies, waits for them, and re-layouts: 3.64 us -> 11.6 us
  Pallas kernels: 128 us -> 133 us
  starting transfers between devices: 3.59 us -> 0 us
    all_gather x1 -> x0, blocking collectives: 14.1 us -> none  [body(): attitude_update = lax.all_gather(own_update, 'sky', axis=1, tiled=True)]
    unnamed x27 -> x31, local copies, waits for them, and re-layouts: 3.14 us -> 11.6 us
    reduce_sum x3 -> x0, other arithmetic: 5.03 us -> none  [tile_rows(): rows.append(jnp.sum(weights * portion[first] * other, axis=-1))]
    pallas_call x4, Pallas kernels: 128 us -> 133 us  [the longest x1 85.9 us: exchange(): pl.pallas_call(functools.partial(exchange_kernel, times, lines), name='ex...]
    sub x2 -> x1, other arithmetic: 4.59 us -> 0.69 us  [body(): knots = (tile_knot - block * span)[None, :]]
    ppermute x2 -> x0, starting transfers between devices: 3.59 us -> none  [passed_along(): lax.ppermute(value, axes, [(source, source + steps) for source in range(f...]
    mul x1 -> x0, other arithmetic: 3.33 us -> none  [tile_rows(): rows.append(jnp.sum(weights * portion[first] * other, axis=-1))]
  transfers between devices with their start and end apart: 2 -> 0, of which waited for: 0 -> 0; matrix products, arithmetic and copies ran while one was open for 1% -> 0% of each run, Pallas kernels for 0% -> 0%
where the time goes in v1:
time: 147 us
  Pallas kernels  133 us (90%)
  local copies, waits for them, and re-layouts  11.6 us (8%)
    pallas_call x1, Pallas kernels, exchange(): pl.pallas_call(functools.partial(exchange_kernel, times, lines), name='ex...  85.9 us
    pallas_call x1, Pallas kernels, local_sums(): pl.pallas_call(functools.partial(sums_kernel, times, owners, tiles_step),...  20.7 us
    pallas_call x1, Pallas kernels, finish(): pl.pallas_call(functools.partial(finish_kernel, times, owners, span), nam...  13.9 us
    pallas_call x1, Pallas kernels, settle(): pl.pallas_call(settle_kernel, name='settle', out_shape=(jax.ShapeDtypeStr...  13.1 us
    unnamed x31, local copies, waits for them, and re-layouts  11.6 us

profile of v1, /device:TPU:0, one launch (start us, length us, event | category | flops | bytes accessed | tf_op | source)
XLA Modules:
  0.0 146.5 jit_solution(13400806239986637792)
XLA Ops:
  0.6 0.7 broadcast_subtract_fusion
  1.3 1.3 copy-done.2
  2.6 0.9 copy-done.4
  3.6 0.9 copy-done.6
  4.5 0.9 copy-done.8
  5.5 0.7 copy-done.10
  6.2 0.7 copy-done.12
  6.9 20.7 %local_sums.1 = f32[20480,128]{1,0:T(8,128)S(1)} custom-call(s32[512]{0:T(512)S(1)} %copy-done.12, s32[1024]{0:T(1024)S(1)} %copy-done.10, f32[512,128]{1,0:T(8,128)S(1)} %copy-done.6, f32[512,128]{1,0:T(8,128)S(1)} %copy-done.4, f32[5,512,128]{2,1,0:T(8,128)S(1)} %copy-done.2, s32[512,128]{1,0:T(8,128)S(1)} %copy-done.8), custom_call_target="tpu_custom_call" | custom-call | tf_op jit(solution)/shard_map/local_sums/pallas_call | solution.py:141
  27.6 0.0 copy-start
  27.6 4.0 %copy-done = f32[20480,128]{1,0:T(8,128)} copy-done((f32[20480,128]{1,0:T(8,128)}, f32[20480,128]{1,0:T(8,128)S(1)}, u32[]{:S(2)}) %copy-start) | copy-done | bytes 10485784
  31.6 0.0 copy-done.1
  31.6 0.0 copy-done.5
  31.6 0.0 copy-start.9
  31.6 0.0 copy-start.11
  31.6 0.0 copy-start.13
  31.6 85.9 %exchange.1 = (f32[5128,128]{1,0:T(8,128)S(1)}, f32[512,128]{1,0:T(8,128)S(1)}) custom-call(f32[4,2,2,1280,128]{4,3,2,1,0:T(8,128)} %bitcast.2, f32[512,128]{1,0:T(8,128)S(1)} %copy-done.5, f32[16,512,128]{2,1,0:T(8,128)S(1)} %copy-done.1), custom_call_target="tpu_custom_call" | custom-call | tf_op jit(solution)/shard_map/exchange/pallas_call | solution.py:415
  117.5 0.0 copy-done.3
  117.5 0.0 copy-done.7
  117.5 0.0 copy-done.9
  117.5 13.1 %settle.1 = (f32[512,128]{1,0:T(8,128)S(1)}, f32[16,128]{1,0:T(8,128)S(1)}) custom-call(s32[512]{0:T(512)S(1)} %copy-done.13, s32[1024]{0:T(1024)S(1)} %copy-done.11, s32[1,512]{1,0:T(1,128)S(1)} %bitcast.3, f32[512,128]{1,0:T(8,128)S(1)} %copy-done.7, f32[512,128]{1,0:T(8,128)S(1)} %copy-done.5, f32[5,512,128]{2,1,0:T(8,128)S(1)} %copy-done.3, ...), custom_call_target="tpu_custom_call" | custom-call | tf_op jit(solution)/shard_map/settle/pallas_call | solution.py:499
  130.6 13.9 %finish.1 = (f32[512,128]{1,0:T(8,128)S(1)}, f32[5,16384]{1,0:T(8,128)S(1)}, f32[4,512]{1,0:T(4,128)S(1)}) custom-call(f32[16,128]{1,0:T(8,128)S(1)} %get-tuple-element.9.sums, s32[1,512]{1,0:T(1,128)S(1)} %bitcast.4, f32[512,128]{1,0:T(8,128)S(1)} %get-tuple-element.10.settled, f32[16,512,128]{2,1,0:T(8,128)S(1)} %copy-done.1, ...), custom_call_target="tpu_custom_call" | custom-call | tf_op jit(solution)/shard_map/finish/pallas_call | solution.py:624
  144.5 0.7 copy.14
  145.2 0.8 copy.15
  146.0 0.6 copy.16
  (12 shorter events, 0.0 us)
Async XLA Ops:
  1.3 1.3 copy-start.2
  2.6 0.9 copy-start.4
  3.6 0.9 copy-start.6
  4.5 0.9 copy-start.8
  5.5 0.7 copy-start.10
  6.2 0.7 copy-start.12
  6.9 24.7 %copy-start.1 = (f32[16,512,128]{2,1,0:T(8,128)S(1)}, f32[16,512,128]{2,1,0:T(8,128)}, u32[]{:S(2)}) copy-start(f32[16,512,128]{2,1,0:T(8,128)} %att.5) | copy-start | bytes 12582916
  6.9 24.7 %copy-start.5 = (f32[512,128]{1,0:T(8,128)S(1)}, f32[512,128]{1,0:T(8,128)}, u32[]{:S(2)}) copy-start(f32[512,128]{1,0:T(8,128)} %weight.5) | copy-start | bytes 786436
  27.6 4.0 %copy-start = (f32[20480,128]{1,0:T(8,128)}, f32[20480,128]{1,0:T(8,128)S(1)}, u32[]{:S(2)}) copy-start(f32[20480,128]{1,0:T(8,128)S(1)} %local_sums.1) | copy-start | bytes 31457284
  31.6 85.9 %copy-start.3 = (f32[5,512,128]{2,1,0:T(8,128)S(1)}, f32[5,512,128]{2,1,0:T(8,128)}, u32[]{:S(2)}) copy-start(f32[5,512,128]{2,1,0:T(8,128)} %parts.3) | copy-start | bytes 3932164
  31.6 85.9 %copy-start.7 = (f32[512,128]{1,0:T(8,128)S(1)}, f32[512,128]{1,0:T(8,128)}, u32[]{:S(2)}) copy-start(f32[512,128]{1,0:T(8,128)} %resid.3) | copy-start | bytes 786436
  31.6 85.9 %copy-start.9 = (s32[512,128]{1,0:T(8,128)S(1)}, s32[512,128]{1,0:T(8,128)}, u32[]{:S(2)}) copy-start(s32[512,128]{1,0:T(8,128)} %index.3) | copy-start | bytes 786436
  31.6 85.9 %copy-start.11 = (s32[1024]{0:T(1024)S(1)}, s32[1024]{0:T(1024)}, u32[]{:S(2)}) copy-start(s32[1024]{0:T(1024)} %slot_ref.3) | copy-start | bytes 12292
  31.6 85.9 %copy-start.13 = (s32[512]{0:T(512)S(1)}, s32[512]{0:T(512)}, u32[]{:S(2)}) copy-start(s32[512]{0:T(512)} %pixel_ref.3) | copy-start | bytes 6148

commit v2 on v1

v2 whole, which is shorter than its diff:
```python
import functools

import jax
import jax.numpy as jnp
from jax import lax
from jax.experimental import pallas as pl
from jax.experimental.pallas import tpu as pltpu
from jax.sharding import PartitionSpec as P

KNOTS_DEV = 512
ROWS = 20
PAD = 24
UPD = 5
LANES = 128
SUB = 8
MIB = 1024 * 1024

SOURCE_PAIRS = tuple(((first, second) for first in range(5) for second in range(first, 5)))
KNOT_PAIRS = tuple(((first, second) for first in range(4) for second in range(first, 4)))


def damped_solve(normal, target, order, pairs):
    entries = {}
    for number, couple in enumerate(pairs):
        entries[couple] = normal[number]
    factor = {}
    for column in range(order):
        pivot_value = entries[column, column] + 1.0
        for earlier in range(column):
            pivot_value = pivot_value - factor[column, earlier] * factor[column, earlier]
        pivot_value = jnp.sqrt(pivot_value)
        factor[column, column] = pivot_value
        for below in range(column + 1, order):
            current = entries[column, below]
            for earlier in range(column):
                current = current - factor[below, earlier] * factor[column, earlier]
            factor[below, column] = current / pivot_value
    forward = []
    for column in range(order):
        current = target[column]
        for earlier in range(column):
            current = current - factor[column, earlier] * forward[earlier]
        forward.append(current / factor[column, column])
    answer = [None] * order
    for column in reversed(range(order)):
        current = forward[column]
        for later in range(column + 1, order):
            current = current - factor[later, column] * answer[later]
        answer[column] = current / factor[column, column]
    return answer


def split_times(times):
    inner = 2 if times % 2 == 0 else 1
    return times // inner, inner


def sums_kernel(
    tiles_step, pixel_hbm, slot_hbm, resid_hbm, weight_hbm, parts_hbm, index_hbm, out,
    pixel_ref, slot_ref, resid, weight, parts, index, stage, prods, sems,
):
    copies = [
        pltpu.make_async_copy(source, target, sems.at[number])
        for number, (source, target) in enumerate(
            [
                (pixel_hbm, pixel_ref),
                (slot_hbm, slot_ref),
                (resid_hbm, resid),
                (weight_hbm, weight),
                (parts_hbm, parts),
                (index_hbm, index),
            ]
        )
    ]
    for copy in copies:
        copy.start()
    tiles = resid.shape[0]
    zero = jnp.zeros((256, LANES), jnp.float32)

    def clear(step, carry):
        out[pl.ds(pl.multiple_of(step * 256, 256), 256), :] = zero
        return carry

    lax.fori_loop(0, out.shape[0] // 256, clear, 0)
    stage[...] = jnp.zeros_like(stage)
    sources = lax.broadcasted_iota(jnp.int32, (SUB, LANES), 0).astype(jnp.float32)
    bands = [
        jnp.concatenate([sources + float(16 * band), sources + float(16 * band + 8)], axis=0).astype(jnp.bfloat16)
        for band in range(LANES // 16)
    ]
    lanes_of = jnp.concatenate(bands, axis=0)
    one = jnp.ones((LANES, LANES), jnp.bfloat16)
    none = jnp.zeros((LANES, LANES), jnp.bfloat16)
    blank = jnp.zeros((2 * PAD, LANES), jnp.bfloat16)
    for copy in copies:
        copy.wait()

    def accumulate(step, slot):
        for j in range(tiles_step):
            start = slot_ref[pixel_ref[step * tiles_step + j]] * ROWS
            values = prods[pl.ds(slot * tiles_step * PAD + j * PAD, PAD), :]
            out[pl.ds(start, ROWS), :] += values[:ROWS]

    def multiply(step, slot):
        for part in range(tiles_step // SUB):
            base = pl.multiple_of(step * tiles_step + part * SUB, SUB)
            here = pl.ds(base, SUB)
            fields = [parts[c, here, :] for c in range(5)]
            scaled = [weight[here, :] * field for field in fields]
            baseline = resid[here, :]
            row = part * SUB * PAD
            for first, second in SOURCE_PAIRS:
                stage[pl.ds(row, SUB, stride=PAD), :] = scaled[first] * fields[second]
                row += 1
            for first in range(5):
                stage[pl.ds(row, SUB, stride=PAD), :] = scaled[first] * baseline
                row += 1
            ids = index[here, :].astype(jnp.float32)
            for j in range(0, SUB, 2):
                row = (part * SUB + j) * PAD
                lhs, hits = [], []
                for side in range(2):
                    values = stage[row + side * PAD : row + (side + 1) * PAD, :]
                    high = values.astype(jnp.bfloat16).astype(jnp.float32)
                    both = jnp.concatenate([high, values - high], axis=0).astype(jnp.bfloat16)
                    lhs.append(jnp.concatenate([both, blank] if side == 0 else [blank, both], axis=1))
                    wide = jnp.broadcast_to(ids[j + side : j + side + 1, :], (16, LANES)).astype(jnp.bfloat16)
                    tall = jnp.concatenate([wide] * (LANES // 16), axis=0)
                    hits.append(jnp.where(lanes_of == tall, one, none))
                got = lax.dot_general(
                    jnp.concatenate(lhs, axis=0),
                    jnp.concatenate(hits, axis=1),
                    (((1,), (1,)), ((), ())),
                    preferred_element_type=jnp.float32,
                )
                for side in range(2):
                    low = 2 * side * PAD
                    prods[pl.ds(slot * tiles_step * PAD + row + side * PAD, PAD), :] = (
                        got[low : low + PAD] + got[low + PAD : low + 2 * PAD]
                    )

    steps = tiles // tiles_step
    multiply(0, 0)

    def pair(step, carry):
        multiply(2 * step + 1, 1)
        accumulate(2 * step, 0)
        multiply(jnp.minimum(2 * step + 2, steps - 1), 0)
        accumulate(2 * step + 1, 1)
        return carry

    lax.fori_loop(0, steps // 2, pair, 0)


def local_sums(tile_pixel, pixel_slot, residual, obs_weight, source_partials, source_index):
    pixels = pixel_slot.shape[0]
    tiles_step = 16
    return pl.pallas_call(
        functools.partial(sums_kernel, tiles_step),
        name="local_sums",
        out_shape=jax.ShapeDtypeStruct((pixels * ROWS, LANES), jnp.float32),
        in_specs=[pl.BlockSpec(memory_space=pltpu.HBM)] * 6,
        out_specs=pl.BlockSpec(memory_space=pltpu.VMEM),
        scratch_shapes=[
            pltpu.SMEM(tile_pixel.shape, jnp.int32),
            pltpu.SMEM(pixel_slot.shape, jnp.int32),
            pltpu.VMEM(residual.shape, jnp.float32),
            pltpu.VMEM(obs_weight.shape, jnp.float32),
            pltpu.VMEM(source_partials.shape, jnp.float32),
            pltpu.VMEM(source_index.shape, jnp.int32),
            pltpu.VMEM((tiles_step * PAD, LANES), jnp.float32),
            pltpu.VMEM((2 * tiles_step * PAD, LANES), jnp.float32),
            pltpu.SemaphoreType.DMA((6,)),
        ],
        compiler_params=pltpu.CompilerParams(vmem_limit_bytes=18 * MIB),
    )(*[pltpu.with_memory_space_constraint(v, pltpu.HBM) for v in (tile_pixel, pixel_slot, residual, obs_weight, source_partials, source_index)])


def add_rows(target, *sources):
    rows = target.shape[0]
    step_rows = next(size for size in range(160, 0, -SUB) if rows % size == 0)

    def one(step, carry):
        here = pl.ds(pl.multiple_of(step * step_rows, step_rows), step_rows)
        total = sources[0][here, :]
        for source in sources[1:]:
            total = total + source[here, :]
        target[here, :] = total
        return carry

    lax.fori_loop(0, rows // step_rows, one, 0)


def square_sums(weight, att, rows, first, last):
    lane = lax.broadcasted_iota(jnp.int32, (SUB, LANES), 1)

    def group(step, carry):
        for part in range(2):
            here = pl.ds(pl.multiple_of(step * 2 * SUB + part * SUB, SUB), SUB)
            scale = weight[here, :]
            total = jnp.zeros((SUB, LANES), jnp.float32)
            for m in range(4):
                fields = [att[4 * m + c, here, :] for c in range(4)]
                scaled = [scale * field for field in fields]
                for number, (a, b) in enumerate(KNOT_PAIRS):
                    value = jnp.sum(scaled[a] * fields[b], axis=1, keepdims=True)
                    total = jnp.where(lane == 16 * m + number, value, total)
            rows[here, :] = total
        return carry

    lax.fori_loop(first, last, group, 0)


def exchange_kernel(
    times, lines, subs, depth, sums, weight, att, table, squares, got0, a1, b1, a2, b2, part, got2, upd, *sems
):
    s0, r0, sa1, ra1, sb1, rb1, sa2, ra2, sb2, rb2, s3, r3, su, ru, st, rt, sd, rd = sems
    outer, inner = split_times(times)
    mesh_ids = pl.DeviceIdType.MESH
    time, sky = lax.axis_index("tm"), lax.axis_index("sky")
    line, core = sky // 2, sky % 2
    mo, mi = time // inner, time % inner
    partner = (time, sky + 1 - 2 * core)
    quarter = a2.shape[2]
    tiles = weight.shape[0]
    inner_at = [lax.rem(mi + step, inner) for step in range(1, inner)]
    outer_at = [lax.rem(mo + step, outer) for step in range(1, outer)]
    inner_peers = [(mo * inner + i, sky) for i in inner_at]
    outer_peers = [(o * inner + mi, sky) for o in outer_at]
    masks = list(range(lines - 1, 0, -1))
    line_of = {mask: jnp.bitwise_xor(line, mask) for mask in range(lines)}
    line_peer = {mask: (time, line_of[mask] * 2 + core) for mask in masks}

    barrier = pltpu.get_barrier_semaphore()
    peers = [partner] + inner_peers + outer_peers + [line_peer[mask] for mask in masks]
    for peer in peers:
        pl.semaphore_signal(barrier, inc=1, device_id=peer, device_id_type=mesh_ids)
    pl.semaphore_wait(barrier, len(peers))

    pending = []

    def send(source, target, send_sem, recv_sem, peer):
        copy = pltpu.make_async_remote_copy(
            src_ref=source, dst_ref=target, send_sem=send_sem, recv_sem=recv_sem,
            device_id=peer, device_id_type=mesh_ids,
        )
        copy.start()
        pending.append(copy)
        return copy

    pieces = [(mask, sub) for mask in masks + [0] for sub in range(subs)]
    count = len(pieces)
    zeroth = [
        send(sums.at[line_of[mask], 1 - core, :, sub], got0.at[k], s0.at[k], r0.at[k], partner)
        for k, (mask, sub) in enumerate(pieces)
    ]
    first_a, first_b, second_a, second_b, third = {}, {}, {}, {}, {}

    def spot_a(k, o, i):
        return got0.at[k, o * inner + i, pl.ds(0, quarter)]

    def spot_b(k, o, i):
        return got0.at[k, o * inner + i, pl.ds(quarter, quarter)]

    def stage_one(k):
        mask, sub = pieces[k]
        zeroth[k].wait_recv()
        first_a[k], first_b[k] = [], []
        for at_o, o in enumerate(outer_at + [mo]):
            for at_i, i in enumerate(inner_at + [mi]):
                t = o * inner + i
                add_rows(got0.at[k, t], got0.at[k, t], sums.at[line_of[mask], core, t, sub])
                if at_i < inner - 1:
                    first_a[k].append(
                        send(
                            spot_a(k, o, i), a1.at[k, at_i, o], sa1.at[k, at_i, at_o], ra1.at[k, at_i, at_o],
                            inner_peers[at_i],
                        )
                    )
                if at_o < outer - 1:
                    first_b[k].append(
                        send(
                            spot_b(k, o, i), b1.at[k, at_o, i], sb1.at[k, at_o, at_i], rb1.at[k, at_o, at_i],
                            outer_peers[at_o],
                        )
                    )

    def stage_two(k):
        for copy in first_a[k]:
            copy.wait_recv()
        second_a[k] = []
        for at_o, o in enumerate(outer_at + [mo]):
            mine = spot_a(k, o, mi)
            add_rows(mine, mine, *[a1.at[k, number, o] for number in range(inner - 1)])
            if at_o < outer - 1:
                second_a[k].append(
                    send(mine, a2.at[k, at_o], sa2.at[k, at_o], ra2.at[k, at_o], outer_peers[at_o])
                )
        for copy in first_b[k]:
            copy.wait_recv()
        second_b[k] = []
        for at_i, i in enumerate(inner_at + [mi]):
            mine = spot_b(k, mo, i)
            add_rows(mine, mine, *[b1.at[k, number, i] for number in range(outer - 1)])
            if at_i < inner - 1:
                second_b[k].append(
                    send(mine, b2.at[k, at_i], sb2.at[k, at_i], rb2.at[k, at_i], inner_peers[at_i])
                )

    def stage_three(k):
        mask, sub = pieces[k]
        for copy in second_a[k]:
            copy.wait_recv()
        add_rows(
            part.at[k, pl.ds(0, quarter)], spot_a(k, mo, mi), *[a2.at[k, number] for number in range(outer - 1)]
        )
        for copy in second_b[k]:
            copy.wait_recv()
        add_rows(
            part.at[k, pl.ds(quarter, quarter)], spot_b(k, mo, mi),
            *[b2.at[k, number] for number in range(inner - 1)],
        )
        if mask:
            third[mask, sub] = send(part.at[k], got2.at[k], s3.at[k], r3.at[k], line_peer[mask])

    run = subs * 2 * quarter // ROWS
    block = run * UPD
    unit = block // subs
    half_unit = unit // 2

    def spot(mask, source_time, sub):
        base = ((line_of[mask] * 2 + core) * times + source_time) * block + sub * unit
        return pl.multiple_of(base, SUB)

    from_line, near, far = {}, {}, {}

    def spread(mask, sub):
        place = table.at[pl.ds(spot(mask, time, sub), unit)]
        if mask:
            from_line[mask, sub].wait_recv()
            held = place
        else:
            held = upd.at[pl.ds(sub * unit, unit)]
        near[mask, sub] = [
            send(held, place, st.at[mask, sub, number], rt.at[mask, sub, number], peer)
            for number, peer in enumerate(inner_peers + outer_peers)
        ]

    def relay(mask, sub):
        far[mask, sub] = []
        number = inner + outer - 2
        for which, copy in enumerate(near[mask, sub]):
            copy.wait_recv()
            if which < inner - 1:
                origin = mo * inner + lax.rem(mi + inner - (which + 1), inner)
                rows, targets = 0, outer_peers
            else:
                origin = lax.rem(mo + outer - (which - inner + 2), outer) * inner + mi
                rows, targets = half_unit, inner_peers
            piece = table.at[pl.ds(pl.multiple_of(spot(mask, origin, sub) + rows, SUB), half_unit)]
            for peer in targets:
                far[mask, sub].append(
                    send(piece, piece, st.at[mask, sub, number], rt.at[mask, sub, number], peer)
                )
                number += 1

    def conclude(mask):
        for sub in range(subs):
            for copy in far[mask, sub]:
                copy.wait_recv()
        place = table.at[pl.ds(spot(mask, 0, 0), times * block)]
        return send(place, place, sd.at[mask], rd.at[mask], partner)

    def own_unit(sub):
        k = pieces.index((0, sub))
        for mask in masks:
            third[mask, sub].wait_recv()
        total = part.at[k]
        add_rows(total, total, *[got2.at[pieces.index((mask, sub))] for mask in masks])

        def solve(step, carry):
            base = step * SUB
            entry = [part[k, pl.ds(base * ROWS + row, SUB, stride=ROWS), :] for row in range(ROWS)]
            answer = damped_solve(entry[:15], entry[15:], 5, SOURCE_PAIRS)
            for c in range(UPD):
                upd[pl.ds(sub * unit + base * UPD + c, SUB, stride=UPD), :] = answer[c]
            return carry

        lax.fori_loop(0, run // subs // SUB, solve, 0)
        ordered = sorted(masks, key=lambda mask: (mask & (mask + 1) != 0, mask))
        for mask in ordered:
            from_line[mask, sub] = send(
                upd.at[pl.ds(sub * unit, unit)], table.at[pl.ds(spot(0, time, sub), unit)],
                su.at[mask, sub], ru.at[mask, sub], line_peer[mask],
            )
        spread(0, sub)
        table[pl.ds(spot(0, time, sub), unit), :] = upd[sub * unit : (sub + 1) * unit, :]

    groups = tiles // (2 * SUB)
    shares = 4
    for k in range(min(depth, count)):
        stage_one(k)
    for k in range(count):
        if k < shares:
            square_sums(weight, att, squares, groups * k // shares, groups * (k + 1) // shares)
        stage_two(k)
        if k + depth < count:
            stage_one(k + depth)
        if k > 0:
            stage_three(k - 1)
            if pieces[k - 1][0] == 0:
                own_unit(pieces[k - 1][1])
    stage_three(count - 1)
    own_unit(subs - 1)

    ordered = [0] + sorted(masks, key=lambda mask: (mask & (mask + 1) != 0, mask))
    sequence = [(mask, sub) for sub in range(subs) for mask in ordered]
    done = {(0, sub) for sub in range(subs)}
    relayed = []
    last = {}
    for at, item in enumerate(sequence):
        if item not in done:
            spread(*item)
        if at >= 2:
            relay(*sequence[at - 2])
            relayed.append(sequence[at - 2])
            if len(relayed) >= 2 and relayed[-2][1] == subs - 1:
                last[relayed[-2][0]] = conclude(relayed[-2][0])
    for item in sequence[-2:]:
        relay(*item)
    for mask in ordered:
        if mask not in last:
            last[mask] = conclude(mask)
    for mask in ordered:
        last[mask].wait_recv()
    for copy in pending:
        copy.wait_send()


def exchange(sums, obs_weight, attitude_partials):
    times, owners = lax.axis_size("tm"), lax.axis_size("sky")
    lines = owners // 2
    outer, inner = split_times(times)
    subs = 2
    total_rows = sums.shape[0]
    unit_rows = total_rows // (owners * times * subs)
    quarter = unit_rows // 2
    pixels = total_rows // ROWS
    block = pixels // (owners * times) * UPD
    tiles = obs_weight.shape[0]
    count = lines * subs
    dma = pltpu.SemaphoreType.DMA
    vmem = pltpu.VMEM
    near = inner + outer - 2
    far = 2 * (inner - 1) * (outer - 1)
    f32 = jnp.float32

    def pair(*shape):
        return [dma(shape), dma(shape)]

    return pl.pallas_call(
        functools.partial(exchange_kernel, times, lines, subs, 3),
        name="exchange",
        out_shape=(
            jax.ShapeDtypeStruct((pixels * UPD + SUB, LANES), f32),
            jax.ShapeDtypeStruct((tiles, LANES), f32),
        ),
        in_specs=[pl.BlockSpec(memory_space=pltpu.VMEM)] * 3,
        out_specs=(pl.BlockSpec(memory_space=pltpu.VMEM),) * 2,
        scratch_shapes=[
            vmem((count, times, unit_rows, LANES), f32),
            vmem((count, max(inner - 1, 1), outer, quarter, LANES), f32),
            vmem((count, max(outer - 1, 1), inner, quarter, LANES), f32),
            vmem((count, max(outer - 1, 1), quarter, LANES), f32),
            vmem((count, max(inner - 1, 1), quarter, LANES), f32),
            vmem((count, unit_rows, LANES), f32),
            vmem((count, unit_rows, LANES), f32),
            vmem((block, LANES), f32),
        ]
        + pair(count)
        + pair(count, max(inner - 1, 1), outer)
        + pair(count, max(outer - 1, 1), inner)
        + pair(count, max(outer - 1, 1))
        + pair(count, max(inner - 1, 1))
        + pair(count)
        + pair(lines, subs)
        + pair(lines, subs, near + far)
        + pair(lines),
        compiler_params=pltpu.CompilerParams(
            collective_id=0, has_side_effects=True, vmem_limit_bytes=24 * MIB
        ),
    )(sums.reshape(lines, 2, times, subs, unit_rows, LANES), obs_weight, attitude_partials)


def thirds(value):
    high = value.astype(jnp.bfloat16)
    rest = value - high.astype(jnp.float32)
    middle = rest.astype(jnp.bfloat16)
    return high, middle, (rest - middle.astype(jnp.float32)).astype(jnp.bfloat16)


def settle_kernel(
    times, owners, span, pixel_hbm, slot_hbm, knots, resid, weight, parts, att, index, table, squares,
    out, source_out, knot_out, pixel_ref, slot_ref, rows, terms, sums, before, mine, after, settles, values, others,
    sp, sl, sa, ra, sb, rb, sc, rc,
):
    mesh_ids = pl.DeviceIdType.MESH
    time, sky = lax.axis_index("tm"), lax.axis_index("sky")
    blocks = times * owners
    block = time * owners + sky
    nxt, prev = lax.rem(block + 1, blocks), lax.rem(block + blocks - 1, blocks)
    next_id, prev_id = (nxt // owners, lax.rem(nxt, owners)), (prev // owners, lax.rem(prev, owners))
    peers = [(time, lax.rem(sky + step, owners)) for step in range(1, owners)]
    barrier = pltpu.get_barrier_semaphore()
    for peer in [next_id, prev_id] + peers:
        pl.semaphore_signal(barrier, inc=1, device_id=peer, device_id_type=mesh_ids)

    pixels_in = pltpu.make_async_copy(pixel_hbm, pixel_ref, sp)
    slots_in = pltpu.make_async_copy(slot_hbm, slot_ref, sl)
    pixels_in.start()
    slots_in.start()
    pixels_in.wait()
    slots_in.wait()
    tiles = resid.shape[0]
    lane = lax.broadcasted_iota(jnp.int32, (SUB, LANES), 1)
    unroll = rows.shape[0]

    def group(step, carry):
        for part in range(unroll):
            base = pl.multiple_of((step * unroll + part) * SUB, SUB)
            here = pl.ds(base, SUB)
            for j in range(SUB):
                seat = slot_ref[pixel_ref[base + j]]
                rows[part, j * SUB : (j + 1) * SUB, :] = table[pl.ds(seat * UPD, SUB), :]
            ids = index[here, :]
            total = None
            for c in range(UPD):
                picked = jnp.take_along_axis(rows[part, pl.ds(c, SUB, stride=SUB), :], ids, axis=1)
                addend = parts[c, here, :] * picked
                total = addend if total is None else total + addend
            settled = resid[here, :] - total
            settles[here, :] = settled
            scaled = weight[here, :] * settled
            term = squares[here, :]
            for m in range(4):
                for c in range(4):
                    value = jnp.sum(scaled * att[4 * m + c, here, :], axis=1, keepdims=True)
                    term = jnp.where(lane == 16 * m + 10 + c, value, term)
            terms[here, :] = term
        return carry

    lax.fori_loop(0, tiles // (SUB * unroll), group, 0)
    knot = lax.broadcasted_iota(jnp.int32, (LANES, tiles), 0) + block * span
    hits = jnp.where(knot == knots[...], 1.0, 0.0).astype(jnp.bfloat16)
    placed = None
    for piece in thirds(terms[...]):
        got = jnp.dot(hits, piece, preferred_element_type=jnp.float32)
        placed = got if placed is None else placed + got
    turned = placed.T
    total = turned[:16]
    for m in range(1, 4):
        total = total + pltpu.roll(turned[16 * m : 16 * m + 16], m, 1)
    sums[...] = total

    pl.semaphore_wait(barrier, owners + 1)
    pending = []

    def send(source, target, send_sem, recv_sem, peer):
        copy = pltpu.make_async_remote_copy(
            src_ref=source, dst_ref=target, send_sem=send_sem, recv_sem=recv_sem,
            device_id=peer, device_id_type=mesh_ids,
        )
        copy.start()
        pending.append(copy)
        return copy

    handed = [send(sums, before, sa, ra, next_id), send(sums, after, sb, rb, prev_id)]
    per_owner = source_out.shape[1] // LANES

    def spread(step, carry):
        for part in range(SUB):
            pixel = step * SUB + part
            place = pl.ds(pl.multiple_of(pixel * LANES, LANES), LANES)
            source_out[:, place] = table[pl.ds((sky * per_owner + pixel) * UPD, UPD), :]
        return carry

    lax.fori_loop(0, per_owner // SUB, spread, 0)
    wide = lax.broadcasted_iota(jnp.int32, (16, LANES), 1)
    for copy in handed:
        copy.wait_recv()
    head = pltpu.roll(before[...], LANES - span, 1)
    tail = pltpu.roll(after[...], span, 1)
    whole = sums[...] + jnp.where((wide < 3) & (block > 0), head, 0.0)
    whole = whole + jnp.where((wide >= span) & (wide < span + 3), tail, 0.0)
    answer = damped_solve(
        [whole[n : n + 1] for n in range(10)], [whole[n : n + 1] for n in range(10, 14)], 4, KNOT_PAIRS
    )
    for c in range(4):
        mine[c : c + 1, :] = answer[c]
        mine[4 + c : 5 + c, :] = answer[c]
    around = [
        send(mine, others.at[sky], sc.at[number], rc.at[number], peer)
        for number, peer in enumerate(peers)
    ]
    others[pl.ds(sky, 1)] = mine[...][None]
    reach = jnp.where(block < blocks - 1, span + 3, span)
    extended = jnp.where(lane < reach, mine[...], 0.0)
    windows = []
    for m in range(0, 4, 2):
        low = extended if m == 0 else pltpu.roll(extended, LANES - m, 1)
        high = pltpu.roll(extended, LANES - m - 1, 1)
        half = lax.broadcasted_iota(jnp.int32, (SUB, LANES), 0) < 4
        windows.append(jnp.where(half, low, high))
    window = jnp.concatenate(windows, axis=0)
    picked = None
    for piece in thirds(window):
        got = jnp.dot(piece, hits, preferred_element_type=jnp.float32)
        picked = got if picked is None else picked + got
    for part in range(tiles // LANES):
        values[part * LANES : (part + 1) * LANES, :] = picked[:, part * LANES : (part + 1) * LANES].T

    def last(step, carry):
        for part in range(unroll):
            here = pl.ds(pl.multiple_of((step * unroll + part) * SUB, SUB), SUB)
            column = values[here, :]
            total = None
            for number in range(16):
                addend = att[number, here, :] * column[:, number : number + 1]
                total = addend if total is None else total + addend
            out[here, :] = settles[here, :] - total
        return carry

    lax.fori_loop(0, tiles // (SUB * unroll), last, 0)
    for copy in around:
        copy.wait_recv()
    each = LANES // span
    for first in range(0, owners, each):
        joined = jnp.where(lane < span, others[first], 0.0)
        for number in range(1, each):
            moved = pltpu.roll(others[first + number], number * span, 1)
            keep = (lane >= number * span) & (lane < (number + 1) * span)
            joined = jnp.where(keep, moved, joined)
        knot_out[:, first * span : first * span + LANES] = joined[:4]
    for copy in pending:
        copy.wait_send()


def settle(tile_pixel, pixel_slot, knots, residual, obs_weight, source_partials, attitude_partials, source_index, table, squares, span):
    times, owners = lax.axis_size("tm"), lax.axis_size("sky")
    tiles = residual.shape[0]
    unroll = 4
    pixels = pixel_slot.shape[0]
    dma = pltpu.SemaphoreType.DMA
    f32 = jnp.float32
    return pl.pallas_call(
        functools.partial(settle_kernel, times, owners, span),
        name="settle",
        out_shape=(
            jax.ShapeDtypeStruct(residual.shape, f32),
            jax.ShapeDtypeStruct((UPD, pixels // owners * LANES), f32),
            jax.ShapeDtypeStruct((4, span * owners), f32),
        ),
        in_specs=[pl.BlockSpec(memory_space=pltpu.HBM)] * 2 + [pl.BlockSpec(memory_space=pltpu.VMEM)] * 8,
        out_specs=(pl.BlockSpec(memory_space=pltpu.VMEM),) * 3,
        scratch_shapes=[
            pltpu.SMEM(tile_pixel.shape, jnp.int32),
            pltpu.SMEM(pixel_slot.shape, jnp.int32),
            pltpu.VMEM((unroll, SUB * SUB, LANES), f32),
            pltpu.VMEM((tiles, LANES), f32),
            pltpu.VMEM((16, LANES), f32),
            pltpu.VMEM((16, LANES), f32),
            pltpu.VMEM((SUB, LANES), f32),
            pltpu.VMEM((16, LANES), f32),
            pltpu.VMEM(residual.shape, f32),
            pltpu.VMEM((tiles, 16), f32),
            pltpu.VMEM((owners, SUB, LANES), f32),
            dma, dma, dma, dma, dma, dma, dma((owners - 1,)), dma((owners - 1,)),
        ],
        compiler_params=pltpu.CompilerParams(
            collective_id=1, has_side_effects=True, vmem_limit_bytes=24 * MIB
        ),
    )(tile_pixel, pixel_slot, knots, residual, obs_weight, source_partials, attitude_partials, source_index, table, squares)


def finish_kernel(*refs):
    count = (len(refs) - 1) // 2
    copies = [
        pltpu.make_async_copy(refs[number], refs[count + number], refs[-1].at[number]) for number in range(count)
    ]
    for copy in copies:
        copy.start()
    for copy in copies:
        copy.wait()


def finish(*results):
    return pl.pallas_call(
        finish_kernel,
        name="finish",
        out_shape=tuple(jax.ShapeDtypeStruct(value.shape, value.dtype) for value in results),
        in_specs=[pl.BlockSpec(memory_space=pltpu.VMEM)] * len(results),
        out_specs=(pl.BlockSpec(memory_space=pltpu.HBM),) * len(results),
        scratch_shapes=[pltpu.SemaphoreType.DMA((len(results),))],
        compiler_params=pltpu.CompilerParams(vmem_limit_bytes=8 * MIB),
    )(*results)


def body(residual, obs_weight, source_partials, attitude_partials, source_index, tile_pixel, tile_knot, pixel_slot):
    span = KNOTS_DEV // lax.axis_size("sky")
    sums = local_sums(tile_pixel, pixel_slot, residual, obs_weight, source_partials, source_index)
    table, squares = exchange(sums, obs_weight, attitude_partials)
    results = settle(
        tile_pixel, pixel_slot, tile_knot[None, :], residual, obs_weight, source_partials,
        attitude_partials, source_index, table, squares, span,
    )
    return finish(*results)


def solution(mesh):
    in_specs = (
        P(("tm", "sky"), None),
        P(("tm", "sky"), None),
        P(None, ("tm", "sky"), None),
        P(None, ("tm", "sky"), None),
        P(("tm", "sky"), None),
        P(("tm", "sky")),
        P(("tm", "sky")),
        P(),
    )
    out_specs = (P(("tm", "sky"), None), P(None, "sky"), P(None, "tm"))
    return jax.shard_map(body, mesh=mesh, in_specs=in_specs, out_specs=out_specs, check_vma=False)
```

time: 147 us -> 104 us (0.71)
  Pallas kernels: 133 us -> 104 us
  local copies, waits for them, and re-layouts: 11.6 us -> 0.05 us
    pallas_call x4, Pallas kernels: 133 us -> 104 us  [the longest x1 79.2 us: exchange(): pl.pallas_call(functools.partial(exchange_kernel, times, lines, subs, 3),...]
    unnamed x31 -> x16, local copies, waits for them, and re-layouts: 11.6 us -> 0.05 us
where the time goes in v2:
time: 104 us
  Pallas kernels  104 us (100%)
    pallas_call x1, Pallas kernels, exchange(): pl.pallas_call(functools.partial(exchange_kernel, times, lines, subs, 3),...  79.2 us
    pallas_call x1, Pallas kernels, settle(): pl.pallas_call(functools.partial(settle_kernel, times, owners, span), nam...  13.3 us
    pallas_call x1, Pallas kernels, local_sums(): pl.pallas_call(functools.partial(sums_kernel, tiles_step), name='local_su...  10.1 us

profile of v2, /device:TPU:0, one launch (start us, length us, event | category | flops | bytes accessed | tf_op | source)
XLA Modules:
  0.0 104.4 jit_solution(4841957185689601967)
XLA Ops:
  0.6 0.0 copy-start
  0.6 0.0 copy-start.2
  0.7 10.1 %local_sums.1 = f32[20480,128]{1,0:T(8,128)S(1)} custom-call(s32[512]{0:T(512)} %pixel_hbm.3, s32[1024]{0:T(1024)} %slot_hbm.3, f32[512,128]{1,0:T(8,128)} %resid.1, f32[512,128]{1,0:T(8,128)} %weight.3, f32[5,512,128]{2,1,0:T(8,128)} %parts.1, s32[512,128]{1,0:T(8,128)} %index.1), custom_call_target="tpu_custom_call" | custom-call | tf_op jit(solution)/shard_map/local_sums/pallas_call | solution.py:158
  10.7 0.0 copy-done
  10.8 0.0 copy-done.2
  10.8 0.0 copy-start.1
  10.8 0.0 copy-start.3
  10.8 0.0 copy-start.4
  10.8 0.0 copy-start.5
  10.8 0.0 copy-start.6
  10.8 0.0 copy-start.7
  10.8 79.2 %exchange.1 = (f32[5128,128]{1,0:T(8,128)S(1)}, f32[512,128]{1,0:T(8,128)S(1)}) custom-call(f32[4,2,4,2,320,128]{5,4,3,2,1,0:T(8,128)S(1)} %bitcast.2, f32[512,128]{1,0:T(8,128)S(1)} %copy-done.2, f32[16,512,128]{2,1,0:T(8,128)S(1)} %copy-done), custom_call_target="tpu_custom_call" | custom-call | tf_op jit(solution)/shard_map/exchange/pallas_call | solution.py:461
  90.1 0.0 copy-done.1
  90.1 0.0 copy-done.3
  90.1 0.0 copy-done.4
  90.1 0.0 copy-done.5
  90.1 0.0 copy-done.6
  90.1 0.0 copy-done.7
  90.1 13.3 %settle.1 = (f32[512,128]{1,0:T(8,128)S(1)}, f32[5,16384]{1,0:T(8,128)S(1)}, f32[4,512]{1,0:T(4,128)S(1)}) custom-call(s32[512]{0:T(512)S(1)} %copy-done.6, s32[1024]{0:T(1024)S(1)} %copy-done.5, s32[1,512]{1,0:T(1,128)S(1)} %bitcast.3, f32[512,128]{1,0:T(8,128)S(1)} %copy-done.3, f32[512,128]{1,0:T(8,128)S(1)} %copy-done.2, f32[5,512,128]{2,1,0:T(8,128)S(1)} %copy-done.1, ...), custom_call_target="tpu_custom_call" | custom-call | tf_op jit(solution)/shard_map/settle/pallas_call | solution.py:655
  103.4 0.9 finish.1
Async XLA Ops:
  0.6 10.1 %copy-start = (f32[16,512,128]{2,1,0:T(8,128)S(1)}, f32[16,512,128]{2,1,0:T(8,128)}, u32[]{:S(2)}) copy-start(f32[16,512,128]{2,1,0:T(8,128)} %att.3) | copy-start | bytes 12582916
  0.6 10.1 %copy-start.2 = (f32[512,128]{1,0:T(8,128)S(1)}, f32[512,128]{1,0:T(8,128)}, u32[]{:S(2)}) copy-start(f32[512,128]{1,0:T(8,128)} %weight.3) | copy-start | bytes 786436
  10.8 79.3 %copy-start.1 = (f32[5,512,128]{2,1,0:T(8,128)S(1)}, f32[5,512,128]{2,1,0:T(8,128)}, u32[]{:S(2)}) copy-start(f32[5,512,128]{2,1,0:T(8,128)} %parts.1) | copy-start | bytes 3932164
  10.8 79.3 %copy-start.3 = (f32[512,128]{1,0:T(8,128)S(1)}, f32[512,128]{1,0:T(8,128)}, u32[]{:S(2)}) copy-start(f32[512,128]{1,0:T(8,128)} %resid.1) | copy-start | bytes 786436
  10.8 79.3 %copy-start.4 = (s32[512,128]{1,0:T(8,128)S(1)}, s32[512,128]{1,0:T(8,128)}, u32[]{:S(2)}) copy-start(s32[512,128]{1,0:T(8,128)} %index.1) | copy-start | bytes 786436
  10.8 79.3 %copy-start.5 = (s32[1024]{0:T(1024)S(1)}, s32[1024]{0:T(1024)}, u32[]{:S(2)}) copy-start(s32[1024]{0:T(1024)} %slot_hbm.3) | copy-start | bytes 12292
  10.8 79.3 %copy-start.6 = (s32[512]{0:T(512)S(1)}, s32[512]{0:T(512)}, u32[]{:S(2)}) copy-start(s32[512]{0:T(512)} %pixel_hbm.3) | copy-start | bytes 6148
  10.8 79.3 %copy-start.7 = (s32[512]{0:T(512)S(1)}, s32[512]{0:T(512)}, u32[]{:S(2)}) copy-start(s32[512]{0:T(512)} %param.14) | copy-start | bytes 6148

commit v3 on v2

--- a/solution.py
+++ b/solution.py
@@ -212,27 +212,33 @@
 
 
 def exchange_kernel(
-    times, lines, subs, depth, sums, weight, att, table, squares, got0, a1, b1, a2, b2, part, got2, upd, *sems
+    times, lines, subs, units, depth, far_rows, sums, weight, att, table, squares,
+    got0, gotz, gz2, a1, b1, a2, b2, part, got2, mine, upd, *sems
 ):
-    s0, r0, sa1, ra1, sb1, rb1, sa2, ra2, sb2, rb2, s3, r3, su, ru, st, rt, sd, rd = sems
+    (
+        s0, r0, sz, rz, sy, ry, sa1, ra1, sb1, rb1, sa2, ra2, sb2, rb2, s3, r3, su, ru, st, rt, sd, rd,
+    ) = sems
     outer, inner = split_times(times)
     mesh_ids = pl.DeviceIdType.MESH
     time, sky = lax.axis_index("tm"), lax.axis_index("sky")
     line, core = sky // 2, sky % 2
     mo, mi = time // inner, time % inner
     partner = (time, sky + 1 - 2 * core)
-    quarter = a2.shape[2]
     tiles = weight.shape[0]
+    rows = got0.shape[2]
     inner_at = [lax.rem(mi + step, inner) for step in range(1, inner)]
     outer_at = [lax.rem(mo + step, outer) for step in range(1, outer)]
     inner_peers = [(mo * inner + i, sky) for i in inner_at]
     outer_peers = [(o * inner + mi, sky) for o in outer_at]
-    masks = list(range(lines - 1, 0, -1))
+    odd = [mask for mask in range(lines - 1, 1, -1) if mask % 2]
+    even = [mask for mask in range(lines - 1, 0, -1) if mask % 2 == 0]
+    masks = odd + even + ([1] if lines > 1 else [])
+    direct = [mask for mask in masks if mask not in odd]
     line_of = {mask: jnp.bitwise_xor(line, mask) for mask in range(lines)}
-    line_peer = {mask: (time, line_of[mask] * 2 + core) for mask in masks}
+    line_peer = {mask: (time, line_of[mask] * 2 + core) for mask in direct}
 
     barrier = pltpu.get_barrier_semaphore()
-    peers = [partner] + inner_peers + outer_peers + [line_peer[mask] for mask in masks]
+    peers = [partner] + inner_peers + outer_peers + [line_peer[mask] for mask in direct]
     for peer in peers:
         pl.semaphore_signal(barrier, inc=1, device_id=peer, device_id_type=mesh_ids)
     pl.semaphore_wait(barrier, len(peers))
@@ -250,82 +256,184 @@
 
     pieces = [(mask, sub) for mask in masks + [0] for sub in range(subs)]
     count = len(pieces)
-    zeroth = [
-        send(sums.at[line_of[mask], 1 - core, :, sub], got0.at[k], s0.at[k], r0.at[k], partner)
-        for k, (mask, sub) in enumerate(pieces)
-    ]
+    zeroth, far_zeroth, far_third = {}, {}, {}
+    far_at = pl.ds(subs * rows, far_rows)
+
+    def stage_zero(k):
+        mask, sub = pieces[k]
+        zeroth[k] = send(
+            sums.at[line_of[mask], 1 - core, :, pl.ds(sub * rows, rows)], got0.at[k], s0.at[k], r0.at[k], partner
+        )
+
+    def far_zero(mask):
+        far_zeroth[mask] = send(
+            sums.at[line_of[mask], 1 - core, :, far_at], gotz.at[mask], sz.at[mask], rz.at[mask], partner
+        )
+
+    far_order = masks + [0]
+    for k in range(max(count, lines)):
+        if k < count:
+            stage_zero(k)
+        if k < lines:
+            far_zero(far_order[k])
+
+    def far_add(mask):
+        far_zeroth[mask].wait_recv()
+        for t in range(times):
+            add_rows(gotz.at[mask, t], gotz.at[mask, t], sums.at[line_of[mask], core, t, far_at])
+
+    def far_send(mask):
+        if mask in even and mask + 1 < lines:
+            far_third[mask + 1].wait_recv()
+            for t in range(times):
+                add_rows(gotz.at[mask, t], gotz.at[mask, t], gz2.at[mask + 1, t])
+        peer = line_peer[mask if mask in direct else 1]
+        far_third[mask] = send(gotz.at[mask], gz2.at[mask], sy.at[mask], ry.at[mask], peer)
+
+    def far_close():
+        for mask in direct:
+            far_third[mask].wait_recv()
+        for t in range(times):
+            add_rows(gotz.at[0, t], gotz.at[0, t], *[gz2.at[mask, t] for mask in direct])
+
     first_a, first_b, second_a, second_b, third = {}, {}, {}, {}, {}
 
+    def held(k):
+        return (got0.at[k], rows // 2) if k < count else (gotz.at[0], far_rows // 2)
+
     def spot_a(k, o, i):
-        return got0.at[k, o * inner + i, pl.ds(0, quarter)]
+        ref, quarter = held(k)
+        return ref.at[o * inner + i, pl.ds(0, quarter)]
 
     def spot_b(k, o, i):
-        return got0.at[k, o * inner + i, pl.ds(quarter, quarter)]
+        ref, quarter = held(k)
+        return ref.at[o * inner + i, pl.ds(quarter, quarter)]
 
     def stage_one(k):
-        mask, sub = pieces[k]
-        zeroth[k].wait_recv()
+        quarter = held(k)[1]
+        size = pl.ds(0, quarter)
+        if k < count:
+            mask, sub = pieces[k]
+            zeroth[k].wait_recv()
+        else:
+            far_close()
         first_a[k], first_b[k] = [], []
         for at_o, o in enumerate(outer_at + [mo]):
             for at_i, i in enumerate(inner_at + [mi]):
                 t = o * inner + i
-                add_rows(got0.at[k, t], got0.at[k, t], sums.at[line_of[mask], core, t, sub])
+                if k < count:
+                    add_rows(
+                        got0.at[k, t], got0.at[k, t],
+                        sums.at[line_of[mask], core, t, pl.ds(sub * rows, rows)],
+                    )
                 if at_i < inner - 1:
                     first_a[k].append(
                         send(
-                            spot_a(k, o, i), a1.at[k, at_i, o], sa1.at[k, at_i, at_o], ra1.at[k, at_i, at_o],
-                            inner_peers[at_i],
+                            spot_a(k, o, i), a1.at[k, at_i, o, size], sa1.at[k, at_i, at_o],
+                            ra1.at[k, at_i, at_o], inner_peers[at_i],
                         )
                     )
                 if at_o < outer - 1:
                     first_b[k].append(
                         send(
-                            spot_b(k, o, i), b1.at[k, at_o, i], sb1.at[k, at_o, at_i], rb1.at[k, at_o, at_i],
-                            outer_peers[at_o],
+                            spot_b(k, o, i), b1.at[k, at_o, i, size], sb1.at[k, at_o, at_i],
+                            rb1.at[k, at_o, at_i], outer_peers[at_o],
                         )
                     )
 
     def stage_two(k):
+        size = pl.ds(0, held(k)[1])
         for copy in first_a[k]:
             copy.wait_recv()
         second_a[k] = []
         for at_o, o in enumerate(outer_at + [mo]):
-            mine = spot_a(k, o, mi)
-            add_rows(mine, mine, *[a1.at[k, number, o] for number in range(inner - 1)])
+            own = spot_a(k, o, mi)
+            add_rows(own, own, *[a1.at[k, number, o, size] for number in range(inner - 1)])
             if at_o < outer - 1:
                 second_a[k].append(
-                    send(mine, a2.at[k, at_o], sa2.at[k, at_o], ra2.at[k, at_o], outer_peers[at_o])
+                    send(own, a2.at[k, at_o, size], sa2.at[k, at_o], ra2.at[k, at_o], outer_peers[at_o])
                 )
         for copy in first_b[k]:
             copy.wait_recv()
         second_b[k] = []
         for at_i, i in enumerate(inner_at + [mi]):
-            mine = spot_b(k, mo, i)
-            add_rows(mine, mine, *[b1.at[k, number, i] for number in range(outer - 1)])
+            own = spot_b(k, mo, i)
+            add_rows(own, own, *[b1.at[k, number, i, size] for number in range(outer - 1)])
             if at_i < inner - 1:
                 second_b[k].append(
-                    send(mine, b2.at[k, at_i], sb2.at[k, at_i], rb2.at[k, at_i], inner_peers[at_i])
+                    send(own, b2.at[k, at_i, size], sb2.at[k, at_i], rb2.at[k, at_i], inner_peers[at_i])
                 )
 
     def stage_three(k):
-        mask, sub = pieces[k]
+        quarter = held(k)[1]
+        size = pl.ds(0, quarter)
+        if k >= count:
+            mask, sub, target, base = 0, subs, mine, subs * rows
+        elif pieces[k][0]:
+            (mask, sub), target, base = pieces[k], part.at[k], 0
+        else:
+            (mask, sub), target, base = pieces[k], mine, pieces[k][1] * rows
+        extra = []
+        if mask in even and mask + 1 < lines:
+            third[mask + 1, sub].wait_recv()
+            extra = [got2.at[pieces.index((mask + 1, sub))]]
+        elif mask == 0 and k < count:
+            for other in direct:
+                third[other, sub].wait_recv()
+            extra = [got2.at[pieces.index((other, sub))] for other in direct]
         for copy in second_a[k]:
             copy.wait_recv()
         add_rows(
-            part.at[k, pl.ds(0, quarter)], spot_a(k, mo, mi), *[a2.at[k, number] for number in range(outer - 1)]
+            target.at[pl.ds(base, quarter)], spot_a(k, mo, mi),
+            *[a2.at[k, number, size] for number in range(outer - 1)],
+            *[ref.at[size] for ref in extra],
         )
         for copy in second_b[k]:
             copy.wait_recv()
         add_rows(
-            part.at[k, pl.ds(quarter, quarter)], spot_b(k, mo, mi),
-            *[b2.at[k, number] for number in range(inner - 1)],
+            target.at[pl.ds(base + quarter, quarter)], spot_b(k, mo, mi),
+            *[b2.at[k, number, size] for number in range(inner - 1)],
+            *[ref.at[pl.ds(quarter, quarter)] for ref in extra],
         )
         if mask:
-            third[mask, sub] = send(part.at[k], got2.at[k], s3.at[k], r3.at[k], line_peer[mask])
-
-    run = subs * 2 * quarter // ROWS
+            peer = line_peer[mask if mask in direct else 1]
+            third[mask, sub] = send(part.at[k], got2.at[k], s3.at[k], r3.at[k], peer)
+
+    groups = tiles // (2 * SUB)
+    shares = 4
+    total = count + 1
+    for at in range(depth):
+        stage_one(at)
+        far_add(far_order[at])
+        if far_order[at] in odd or far_order[at] == 1:
+            far_send(far_order[at])
+    waiting = [mask for mask in far_order[depth:]]
+    late = [mask for mask in far_order[:depth] if mask in even]
+    for k in range(total):
+        if k < shares:
+            square_sums(weight, att, squares, groups * k // shares, groups * (k + 1) // shares)
+        stage_two(k)
+        if k + depth < total:
+            stage_one(k + depth)
+        if waiting and k < depth:
+            for mask in waiting:
+                far_add(mask)
+                if mask in odd or mask == 1:
+                    far_send(mask)
+                elif mask in even:
+                    late.append(mask)
+            waiting = []
+        elif late:
+            for mask in late:
+                far_send(mask)
+            late = []
+        if k > 0:
+            stage_three(k - 1)
+    stage_three(total - 1)
+
+    run = mine.shape[0] // ROWS
     block = run * UPD
-    unit = block // subs
+    unit = block // units
     half_unit = unit // 2
 
     def spot(mask, source_time, sub):
@@ -336,13 +444,17 @@
 
     def spread(mask, sub):
         place = table.at[pl.ds(spot(mask, time, sub), unit)]
+        held_in = place
         if mask:
             from_line[mask, sub].wait_recv()
-            held = place
+            if mask in even and mask + 1 < lines:
+                from_line[mask + 1, sub] = send(
+                    place, place, su.at[mask + 1, sub], ru.at[mask + 1, sub], line_peer[1]
+                )
         else:
-            held = upd.at[pl.ds(sub * unit, unit)]
+            held_in = upd.at[pl.ds(sub * unit, unit)]
         near[mask, sub] = [
-            send(held, place, st.at[mask, sub, number], rt.at[mask, sub, number], peer)
+            send(held_in, place, st.at[mask, sub, number], rt.at[mask, sub, number], peer)
             for number, peer in enumerate(inner_peers + outer_peers)
         ]
 
@@ -353,11 +465,11 @@
             copy.wait_recv()
             if which < inner - 1:
                 origin = mo * inner + lax.rem(mi + inner - (which + 1), inner)
-                rows, targets = 0, outer_peers
+                start, targets = 0, outer_peers
             else:
                 origin = lax.rem(mo + outer - (which - inner + 2), outer) * inner + mi
-                rows, targets = half_unit, inner_peers
-            piece = table.at[pl.ds(pl.multiple_of(spot(mask, origin, sub) + rows, SUB), half_unit)]
+                start, targets = half_unit, inner_peers
+            piece = table.at[pl.ds(pl.multiple_of(spot(mask, origin, sub) + start, SUB), half_unit)]
             for peer in targets:
                 far[mask, sub].append(
                     send(piece, piece, st.at[mask, sub, number], rt.at[mask, sub, number], peer)
@@ -365,30 +477,25 @@
                 number += 1
 
     def conclude(mask):
-        for sub in range(subs):
+        for sub in range(units):
             for copy in far[mask, sub]:
                 copy.wait_recv()
         place = table.at[pl.ds(spot(mask, 0, 0), times * block)]
         return send(place, place, sd.at[mask], rd.at[mask], partner)
 
-    def own_unit(sub):
-        k = pieces.index((0, sub))
-        for mask in masks:
-            third[mask, sub].wait_recv()
-        total = part.at[k]
-        add_rows(total, total, *[got2.at[pieces.index((mask, sub))] for mask in masks])
+    for sub in range(units):
+        pixels = run // units
 
         def solve(step, carry):
-            base = step * SUB
-            entry = [part[k, pl.ds(base * ROWS + row, SUB, stride=ROWS), :] for row in range(ROWS)]
+            base = sub * pixels + step * SUB
+            entry = [mine[pl.ds(base * ROWS + row, SUB, stride=ROWS), :] for row in range(ROWS)]
             answer = damped_solve(entry[:15], entry[15:], 5, SOURCE_PAIRS)
             for c in range(UPD):
-                upd[pl.ds(sub * unit + base * UPD + c, SUB, stride=UPD), :] = answer[c]
+                upd[pl.ds(base * UPD + c, SUB, stride=UPD), :] = answer[c]
             return carry
 
-        lax.fori_loop(0, run // subs // SUB, solve, 0)
-        ordered = sorted(masks, key=lambda mask: (mask & (mask + 1) != 0, mask))
-        for mask in ordered:
+        lax.fori_loop(0, pixels // SUB, solve, 0)
+        for mask in even + [1]:
             from_line[mask, sub] = send(
                 upd.at[pl.ds(sub * unit, unit)], table.at[pl.ds(spot(0, time, sub), unit)],
                 su.at[mask, sub], ru.at[mask, sub], line_peer[mask],
@@ -396,36 +503,16 @@
         spread(0, sub)
         table[pl.ds(spot(0, time, sub), unit), :] = upd[sub * unit : (sub + 1) * unit, :]
 
-    groups = tiles // (2 * SUB)
-    shares = 4
-    for k in range(min(depth, count)):
-        stage_one(k)
-    for k in range(count):
-        if k < shares:
-            square_sums(weight, att, squares, groups * k // shares, groups * (k + 1) // shares)
-        stage_two(k)
-        if k + depth < count:
-            stage_one(k + depth)
-        if k > 0:
-            stage_three(k - 1)
-            if pieces[k - 1][0] == 0:
-                own_unit(pieces[k - 1][1])
-    stage_three(count - 1)
-    own_unit(subs - 1)
-
-    ordered = [0] + sorted(masks, key=lambda mask: (mask & (mask + 1) != 0, mask))
-    sequence = [(mask, sub) for sub in range(subs) for mask in ordered]
-    done = {(0, sub) for sub in range(subs)}
-    relayed = []
+    ordered = [0, 1] + even[::-1] + odd[::-1]
+    sequence = [(mask, sub) for mask in ordered for sub in range(units)]
     last = {}
     for at, item in enumerate(sequence):
-        if item not in done:
+        if item[0]:
             spread(*item)
         if at >= 2:
             relay(*sequence[at - 2])
-            relayed.append(sequence[at - 2])
-            if len(relayed) >= 2 and relayed[-2][1] == subs - 1:
-                last[relayed[-2][0]] = conclude(relayed[-2][0])
+        if at >= 3 and sequence[at - 3][1] == units - 1:
+            last[sequence[at - 3][0]] = conclude(sequence[at - 3][0])
     for item in sequence[-2:]:
         relay(*item)
     for mask in ordered:
@@ -441,14 +528,19 @@
     times, owners = lax.axis_size("tm"), lax.axis_size("sky")
     lines = owners // 2
     outer, inner = split_times(times)
-    subs = 2
     total_rows = sums.shape[0]
-    unit_rows = total_rows // (owners * times * subs)
-    quarter = unit_rows // 2
+    chunk = total_rows // (owners * times)
     pixels = total_rows // ROWS
-    block = pixels // (owners * times) * UPD
+    block = chunk // ROWS * UPD
+    far_rows = chunk // 4
+    rest = chunk - far_rows
+    subs = 2 if rest % 32 == 0 else 1
+    units = 2 if block % 32 == 0 else 1
+    rows = rest // subs
+    quarter = max(rows, far_rows) // 2
     tiles = obs_weight.shape[0]
     count = lines * subs
+    total = count + 1
     dma = pltpu.SemaphoreType.DMA
     vmem = pltpu.VMEM
     near = inner + outer - 2
@@ -459,7 +551,7 @@
         return [dma(shape), dma(shape)]
 
     return pl.pallas_call(
-        functools.partial(exchange_kernel, times, lines, subs, 3),
+        functools.partial(exchange_kernel, times, lines, subs, units, 2, far_rows),
         name="exchange",
         out_shape=(
             jax.ShapeDtypeStruct((pixels * UPD + SUB, LANES), f32),
@@ -468,28 +560,33 @@
         in_specs=[pl.BlockSpec(memory_space=pltpu.VMEM)] * 3,
         out_specs=(pl.BlockSpec(memory_space=pltpu.VMEM),) * 2,
         scratch_shapes=[
-            vmem((count, times, unit_rows, LANES), f32),
-            vmem((count, max(inner - 1, 1), outer, quarter, LANES), f32),
-            vmem((count, max(outer - 1, 1), inner, quarter, LANES), f32),
-            vmem((count, max(outer - 1, 1), quarter, LANES), f32),
-            vmem((count, max(inner - 1, 1), quarter, LANES), f32),
-            vmem((count, unit_rows, LANES), f32),
-            vmem((count, unit_rows, LANES), f32),
+            vmem((count, times, rows, LANES), f32),
+            vmem((lines, times, far_rows, LANES), f32),
+            vmem((lines, times, far_rows, LANES), f32),
+            vmem((total, max(inner - 1, 1), outer, quarter, LANES), f32),
+            vmem((total, max(outer - 1, 1), inner, quarter, LANES), f32),
+            vmem((total, max(outer - 1, 1), quarter, LANES), f32),
+            vmem((total, max(inner - 1, 1), quarter, LANES), f32),
+            vmem((count, rows, LANES), f32),
+            vmem((count, rows, LANES), f32),
+            vmem((chunk, LANES), f32),
             vmem((block, LANES), f32),
         ]
         + pair(count)
-        + pair(count, max(inner - 1, 1), outer)
-        + pair(count, max(outer - 1, 1), inner)
-        + pair(count, max(outer - 1, 1))
-        + pair(count, max(inner - 1, 1))
+        + pair(lines)
+        + pair(lines)
+        + pair(total, max(inner - 1, 1), outer)
+        + pair(total, max(outer - 1, 1), inner)
+        + pair(total, max(outer - 1, 1))
+        + pair(total, max(inner - 1, 1))
         + pair(count)
-        + pair(lines, subs)
-        + pair(lines, subs, near + far)
+        + pair(lines, units)
+        + pair(lines, units, near + far)
         + pair(lines),
         compiler_params=pltpu.CompilerParams(
             collective_id=0, has_side_effects=True, vmem_limit_bytes=24 * MIB
         ),
-    )(sums.reshape(lines, 2, times, subs, unit_rows, LANES), obs_weight, attitude_partials)
+    )(sums.reshape(lines, 2, times, chunk, LANES), obs_weight, attitude_partials)
 
 
 def thirds(value):
@@ -648,7 +745,7 @@
 def settle(tile_pixel, pixel_slot, knots, residual, obs_weight, source_partials, attitude_partials, source_index, table, squares, span):
     times, owners = lax.axis_size("tm"), lax.axis_size("sky")
     tiles = residual.shape[0]
-    unroll = 4
+    unroll = 8
     pixels = pixel_slot.shape[0]
     dma = pltpu.SemaphoreType.DMA
     f32 = jnp.float32

time: 104 us -> 96.5 us (0.928)
  Pallas kernels: 104 us -> 95.6 us
    pallas_call x1, Pallas kernels: 79.2 us -> 71 us  [exchange(): pl.pallas_call(functools.partial(exchange_kernel, times, lines, subs, uni...]
where the time goes in v3:
time: 96.5 us; the launch traced here: 96.4 us
  Pallas kernels  95.6 us (99%)
    pallas_call x1, Pallas kernels, exchange(): pl.pallas_call(functools.partial(exchange_kernel, times, lines, subs, uni...  71 us
    pallas_call x1, Pallas kernels, settle(): pl.pallas_call(functools.partial(settle_kernel, times, owners, span), nam...  13.6 us
    pallas_call x1, Pallas kernels, local_sums(): pl.pallas_call(functools.partial(sums_kernel, tiles_step), name='local_su...  10.1 us

profile of v3, /device:TPU:0, one launch (start us, length us, event | category | flops | bytes accessed | tf_op | source)
XLA Modules:
  0.0 96.4 jit_solution(17418274672616642159)
XLA Ops:
  0.6 0.0 copy-start
  0.6 0.0 copy-start.2
  0.7 10.1 %local_sums.1 = f32[20480,128]{1,0:T(8,128)S(1)} custom-call(s32[512]{0:T(512)} %pixel_hbm.3, s32[1024]{0:T(1024)} %slot_hbm.3, f32[512,128]{1,0:T(8,128)} %resid.1, f32[512,128]{1,0:T(8,128)} %weight.3, f32[5,512,128]{2,1,0:T(8,128)} %parts.1, s32[512,128]{1,0:T(8,128)} %index.1), custom_call_target="tpu_custom_call" | custom-call | tf_op jit(solution)/shard_map/local_sums/pallas_call | solution.py:158
  10.7 0.0 copy-done
  10.7 0.0 copy-done.2
  10.8 0.0 copy-start.1
  10.8 0.0 copy-start.3
  10.8 0.0 copy-start.4
  10.8 0.0 copy-start.5
  10.8 0.0 copy-start.6
  10.8 0.0 copy-start.7
  10.8 71.0 %exchange.1 = (f32[5128,128]{1,0:T(8,128)S(1)}, f32[512,128]{1,0:T(8,128)S(1)}) custom-call(f32[4,2,4,640,128]{4,3,2,1,0:T(8,128)S(1)} %bitcast.2, f32[512,128]{1,0:T(8,128)S(1)} %copy-done.2, f32[16,512,128]{2,1,0:T(8,128)S(1)} %copy-done), custom_call_target="tpu_custom_call" | custom-call | tf_op jit(solution)/shard_map/exchange/pallas_call | solution.py:553
  81.8 0.0 copy-done.1
  81.8 0.0 copy-done.3
  81.9 0.0 copy-done.4
  81.9 0.0 copy-done.5
  81.9 0.0 copy-done.6
  81.9 0.0 copy-done.7
  81.9 13.6 %settle.1 = (f32[512,128]{1,0:T(8,128)S(1)}, f32[5,16384]{1,0:T(8,128)S(1)}, f32[4,512]{1,0:T(4,128)S(1)}) custom-call(s32[512]{0:T(512)S(1)} %copy-done.6, s32[1024]{0:T(1024)S(1)} %copy-done.5, s32[1,512]{1,0:T(1,128)S(1)} %bitcast.3, f32[512,128]{1,0:T(8,128)S(1)} %copy-done.3, f32[512,128]{1,0:T(8,128)S(1)} %copy-done.2, f32[5,512,128]{2,1,0:T(8,128)S(1)} %copy-done.1, ...), custom_call_target="tpu_custom_call" | custom-call | tf_op jit(solution)/shard_map/settle/pallas_call | solution.py:752
  95.5 0.9 finish.1
Async XLA Ops:
  0.6 10.1 %copy-start = (f32[16,512,128]{2,1,0:T(8,128)S(1)}, f32[16,512,128]{2,1,0:T(8,128)}, u32[]{:S(2)}) copy-start(f32[16,512,128]{2,1,0:T(8,128)} %att.3) | copy-start | bytes 12582916
  0.6 10.1 %copy-start.2 = (f32[512,128]{1,0:T(8,128)S(1)}, f32[512,128]{1,0:T(8,128)}, u32[]{:S(2)}) copy-start(f32[512,128]{1,0:T(8,128)} %weight.3) | copy-start | bytes 786436
  10.8 71.1 %copy-start.1 = (f32[5,512,128]{2,1,0:T(8,128)S(1)}, f32[5,512,128]{2,1,0:T(8,128)}, u32[]{:S(2)}) copy-start(f32[5,512,128]{2,1,0:T(8,128)} %parts.1) | copy-start | bytes 3932164
  10.8 71.1 %copy-start.3 = (f32[512,128]{1,0:T(8,128)S(1)}, f32[512,128]{1,0:T(8,128)}, u32[]{:S(2)}) copy-start(f32[512,128]{1,0:T(8,128)} %resid.1) | copy-start | bytes 786436
  10.8 71.1 %copy-start.4 = (s32[512,128]{1,0:T(8,128)S(1)}, s32[512,128]{1,0:T(8,128)}, u32[]{:S(2)}) copy-start(s32[512,128]{1,0:T(8,128)} %index.1) | copy-start | bytes 786436
  10.8 71.1 %copy-start.5 = (s32[1024]{0:T(1024)S(1)}, s32[1024]{0:T(1024)}, u32[]{:S(2)}) copy-start(s32[1024]{0:T(1024)} %slot_hbm.3) | copy-start | bytes 12292
  10.8 71.1 %copy-start.6 = (s32[512]{0:T(512)S(1)}, s32[512]{0:T(512)}, u32[]{:S(2)}) copy-start(s32[512]{0:T(512)} %pixel_hbm.3) | copy-start | bytes 6148
  10.8 71.1 %copy-start.7 = (s32[512]{0:T(512)S(1)}, s32[512]{0:T(512)}, u32[]{:S(2)}) copy-start(s32[512]{0:T(512)} %param.14) | copy-start | bytes 6148

commit v4 on v3

--- a/solution.py
+++ b/solution.py
@@ -23,30 +23,29 @@
     entries = {}
     for number, couple in enumerate(pairs):
         entries[couple] = normal[number]
-    factor = {}
+    factor, inverse = {}, []
     for column in range(order):
         pivot_value = entries[column, column] + 1.0
         for earlier in range(column):
             pivot_value = pivot_value - factor[column, earlier] * factor[column, earlier]
-        pivot_value = jnp.sqrt(pivot_value)
-        factor[column, column] = pivot_value
+        inverse.append(1.0 / jnp.sqrt(pivot_value))
         for below in range(column + 1, order):
             current = entries[column, below]
             for earlier in range(column):
                 current = current - factor[below, earlier] * factor[column, earlier]
-            factor[below, column] = current / pivot_value
+            factor[below, column] = current * inverse[column]
     forward = []
     for column in range(order):
         current = target[column]
         for earlier in range(column):
             current = current - factor[column, earlier] * forward[earlier]
-        forward.append(current / factor[column, column])
+        forward.append(current * inverse[column])
     answer = [None] * order
     for column in reversed(range(order)):
         current = forward[column]
         for later in range(column + 1, order):
             current = current - factor[later, column] * answer[later]
-        answer[column] = current / factor[column, column]
+        answer[column] = current * inverse[column]
     return answer
 
 
@@ -154,7 +153,7 @@
 
 def local_sums(tile_pixel, pixel_slot, residual, obs_weight, source_partials, source_index):
     pixels = pixel_slot.shape[0]
-    tiles_step = 16
+    tiles_step = 32
     return pl.pallas_call(
         functools.partial(sums_kernel, tiles_step),
         name="local_sums",
@@ -486,15 +485,15 @@
     for sub in range(units):
         pixels = run // units
 
-        def solve(step, carry):
-            base = sub * pixels + step * SUB
-            entry = [mine[pl.ds(base * ROWS + row, SUB, stride=ROWS), :] for row in range(ROWS)]
-            answer = damped_solve(entry[:15], entry[15:], 5, SOURCE_PAIRS)
-            for c in range(UPD):
-                upd[pl.ds(base * UPD + c, SUB, stride=UPD), :] = answer[c]
-            return carry
-
-        lax.fori_loop(0, pixels // SUB, solve, 0)
+        starts = [sub * pixels + start for start in range(0, pixels, SUB)]
+        entry = [
+            jnp.concatenate([mine[pl.ds(start * ROWS + row, SUB, stride=ROWS), :] for start in starts], axis=0)
+            for row in range(ROWS)
+        ]
+        answer = damped_solve(entry[:15], entry[15:], 5, SOURCE_PAIRS)
+        for c in range(UPD):
+            for number, start in enumerate(starts):
+                upd[pl.ds(start * UPD + c, SUB, stride=UPD), :] = answer[c][number * SUB : (number + 1) * SUB]
         for mask in even + [1]:
             from_line[mask, sub] = send(
                 upd.at[pl.ds(sub * unit, unit)], table.at[pl.ds(spot(0, time, sub), unit)],
@@ -504,22 +503,20 @@
         table[pl.ds(spot(0, time, sub), unit), :] = upd[sub * unit : (sub + 1) * unit, :]
 
     ordered = [0, 1] + even[::-1] + odd[::-1]
-    sequence = [(mask, sub) for mask in ordered for sub in range(units)]
-    last = {}
-    for at, item in enumerate(sequence):
-        if item[0]:
-            spread(*item)
-        if at >= 2:
-            relay(*sequence[at - 2])
-        if at >= 3 and sequence[at - 3][1] == units - 1:
-            last[sequence[at - 3][0]] = conclude(sequence[at - 3][0])
-    for item in sequence[-2:]:
-        relay(*item)
-    for mask in ordered:
-        if mask not in last:
-            last[mask] = conclude(mask)
-    for mask in ordered:
-        last[mask].wait_recv()
+    def each(step, *group):
+        for mask in group:
+            for sub in range(units):
+                step(mask, sub)
+
+    each(spread, 1, *even[::-1])
+    each(relay, 0, 1)
+    each(spread, *odd[::-1])
+    each(relay, *even[::-1])
+    last = [conclude(0)]
+    each(relay, *odd[::-1])
+    last += [conclude(mask) for mask in ordered[1:]]
+    for copy in last:
+        copy.wait_recv()
     for copy in pending:
         copy.wait_send()
 

time: 96.5 us -> 93.3 us (0.967)
  Pallas kernels: 95.6 us -> 92.2 us
    pallas_call x1, Pallas kernels: 71 us -> 67.9 us  [exchange(): pl.pallas_call(functools.partial(exchange_kernel, times, lines, subs, uni...]
where the time goes in v4:
time: 93.3 us; the launch traced here: 93.1 us
  Pallas kernels  92.2 us (99%)
    pallas_call x1, Pallas kernels, exchange(): pl.pallas_call(functools.partial(exchange_kernel, times, lines, subs, uni...  67.9 us
    pallas_call x1, Pallas kernels, settle(): pl.pallas_call(functools.partial(settle_kernel, times, owners, span), nam...  14.3 us
    pallas_call x1, Pallas kernels, local_sums(): pl.pallas_call(functools.partial(sums_kernel, tiles_step), name='local_su...  9.16 us

profile of v4, /device:TPU:0, one launch (start us, length us, event | category | flops | bytes accessed | tf_op | source)
XLA Modules:
  0.0 93.1 jit_solution(2830884292108211319)
XLA Ops:
  0.6 0.0 copy-start
  0.6 0.0 copy-start.2
  0.7 9.2 %local_sums.1 = f32[20480,128]{1,0:T(8,128)S(1)} custom-call(s32[512]{0:T(512)} %pixel_hbm.3, s32[1024]{0:T(1024)} %slot_hbm.3, f32[512,128]{1,0:T(8,128)} %resid.1, f32[512,128]{1,0:T(8,128)} %weight.3, f32[5,512,128]{2,1,0:T(8,128)} %parts.1, s32[512,128]{1,0:T(8,128)} %index.1), custom_call_target="tpu_custom_call" | custom-call | tf_op jit(solution)/shard_map/local_sums/pallas_call | solution.py:157
  9.8 0.0 copy-done
  9.8 0.0 copy-done.2
  9.8 0.0 copy-start.1
  9.8 0.0 copy-start.3
  9.9 0.0 copy-start.4
  9.9 0.0 copy-start.5
  9.9 0.0 copy-start.6
  9.9 0.0 copy-start.7
  9.9 67.9 %exchange.1 = (f32[5128,128]{1,0:T(8,128)S(1)}, f32[512,128]{1,0:T(8,128)S(1)}) custom-call(f32[4,2,4,640,128]{4,3,2,1,0:T(8,128)S(1)} %bitcast.2, f32[512,128]{1,0:T(8,128)S(1)} %copy-done.2, f32[16,512,128]{2,1,0:T(8,128)S(1)} %copy-done), custom_call_target="tpu_custom_call" | custom-call | tf_op jit(solution)/shard_map/exchange/pallas_call | solution.py:550
  77.8 0.0 copy-done.1
  77.8 0.0 copy-done.3
  77.8 0.0 copy-done.4
  77.8 0.0 copy-done.5
  77.8 0.0 copy-done.6
  77.8 0.0 copy-done.7
  77.9 14.3 %settle.1 = (f32[512,128]{1,0:T(8,128)S(1)}, f32[5,16384]{1,0:T(8,128)S(1)}, f32[4,512]{1,0:T(4,128)S(1)}) custom-call(s32[512]{0:T(512)S(1)} %copy-done.6, s32[1024]{0:T(1024)S(1)} %copy-done.5, s32[1,512]{1,0:T(1,128)S(1)} %bitcast.3, f32[512,128]{1,0:T(8,128)S(1)} %copy-done.3, f32[512,128]{1,0:T(8,128)S(1)} %copy-done.2, f32[5,512,128]{2,1,0:T(8,128)S(1)} %copy-done.1, ...), custom_call_target="tpu_custom_call" | custom-call | tf_op jit(solution)/shard_map/settle/pallas_call | solution.py:749
  92.1 0.9 finish.1
Async XLA Ops:
  0.6 9.2 %copy-start = (f32[16,512,128]{2,1,0:T(8,128)S(1)}, f32[16,512,128]{2,1,0:T(8,128)}, u32[]{:S(2)}) copy-start(f32[16,512,128]{2,1,0:T(8,128)} %att.3) | copy-start | bytes 12582916
  0.6 9.2 %copy-start.2 = (f32[512,128]{1,0:T(8,128)S(1)}, f32[512,128]{1,0:T(8,128)}, u32[]{:S(2)}) copy-start(f32[512,128]{1,0:T(8,128)} %weight.3) | copy-start | bytes 786436
  9.8 68.0 %copy-start.1 = (f32[5,512,128]{2,1,0:T(8,128)S(1)}, f32[5,512,128]{2,1,0:T(8,128)}, u32[]{:S(2)}) copy-start(f32[5,512,128]{2,1,0:T(8,128)} %parts.1) | copy-start | bytes 3932164
  9.8 68.0 %copy-start.3 = (f32[512,128]{1,0:T(8,128)S(1)}, f32[512,128]{1,0:T(8,128)}, u32[]{:S(2)}) copy-start(f32[512,128]{1,0:T(8,128)} %resid.1) | copy-start | bytes 786436
  9.9 68.0 %copy-start.4 = (s32[512,128]{1,0:T(8,128)S(1)}, s32[512,128]{1,0:T(8,128)}, u32[]{:S(2)}) copy-start(s32[512,128]{1,0:T(8,128)} %index.1) | copy-start | bytes 786436
  9.9 68.0 %copy-start.5 = (s32[1024]{0:T(1024)S(1)}, s32[1024]{0:T(1024)}, u32[]{:S(2)}) copy-start(s32[1024]{0:T(1024)} %slot_hbm.3) | copy-start | bytes 12292
  9.9 68.0 %copy-start.6 = (s32[512]{0:T(512)S(1)}, s32[512]{0:T(512)}, u32[]{:S(2)}) copy-start(s32[512]{0:T(512)} %pixel_hbm.3) | copy-start | bytes 6148
  9.9 68.0 %copy-start.7 = (s32[512]{0:T(512)S(1)}, s32[512]{0:T(512)}, u32[]{:S(2)}) copy-start(s32[512]{0:T(512)} %param.14) | copy-start | bytes 6148

commit v5 on v4

--- a/solution.py
+++ b/solution.py
@@ -153,7 +153,7 @@
 
 def local_sums(tile_pixel, pixel_slot, residual, obs_weight, source_partials, source_index):
     pixels = pixel_slot.shape[0]
-    tiles_step = 32
+    tiles_step = 64
     return pl.pallas_call(
         functools.partial(sums_kernel, tiles_step),
         name="local_sums",
@@ -529,7 +529,7 @@
     chunk = total_rows // (owners * times)
     pixels = total_rows // ROWS
     block = chunk // ROWS * UPD
-    far_rows = chunk // 4
+    far_rows = chunk // 5
     rest = chunk - far_rows
     subs = 2 if rest % 32 == 0 else 1
     units = 2 if block % 32 == 0 else 1
@@ -595,8 +595,8 @@
 
 def settle_kernel(
     times, owners, span, pixel_hbm, slot_hbm, knots, resid, weight, parts, att, index, table, squares,
-    out, source_out, knot_out, pixel_ref, slot_ref, rows, terms, sums, before, mine, after, settles, values, others,
-    sp, sl, sa, ra, sb, rb, sc, rc,
+    out, source_out, knot_out, pixel_ref, slot_ref, rows, terms, sums, before, mine, after, settles, values, others, gathered,
+    sp, sl, sa, ra, sb, rb, sc, rc, sd, rd,
 ):
     mesh_ids = pl.DeviceIdType.MESH
     time, sky = lax.axis_index("tm"), lax.axis_index("sky")
@@ -606,7 +606,8 @@
     next_id, prev_id = (nxt // owners, lax.rem(nxt, owners)), (prev // owners, lax.rem(prev, owners))
     peers = [(time, lax.rem(sky + step, owners)) for step in range(1, owners)]
     barrier = pltpu.get_barrier_semaphore()
-    for peer in [next_id, prev_id] + peers:
+    edge_id = (lax.rem(time + times - 1, times), owners - 1)
+    for peer in [next_id, prev_id, edge_id] + peers:
         pl.semaphore_signal(barrier, inc=1, device_id=peer, device_id_type=mesh_ids)
 
     pixels_in = pltpu.make_async_copy(pixel_hbm, pixel_ref, sp)
@@ -656,7 +657,8 @@
         total = total + pltpu.roll(turned[16 * m : 16 * m + 16], m, 1)
     sums[...] = total
 
-    pl.semaphore_wait(barrier, owners + 1)
+    last_of = sky == owners - 1
+    pl.semaphore_wait(barrier, owners + 1 + jnp.where(last_of, owners, 0))
     pending = []
 
     def send(source, target, send_sem, recv_sem, peer):
@@ -669,6 +671,24 @@
         return copy
 
     handed = [send(sums, before, sa, ra, next_id), send(sums, after, sb, rb, prev_id)]
+    around = [
+        send(sums, gathered.at[pl.ds((sky + 1) * 16, 16)], sc.at[number], rc.at[number], peer)
+        for number, peer in enumerate(peers)
+    ]
+    edges = [
+        pltpu.make_async_remote_copy(
+            src_ref=sums, dst_ref=gathered.at[pl.ds(0, 16)], send_sem=sd.at[number], recv_sem=rd,
+            device_id=(lax.rem(time + 1, times), number), device_id_type=mesh_ids,
+        )
+        for number in range(owners)
+    ]
+
+    @pl.when(last_of)
+    def _():
+        for copy in edges:
+            copy.start()
+
+    gathered[pl.ds(pl.multiple_of((sky + 1) * 16, 16), 16), :] = sums[...]
     per_owner = source_out.shape[1] // LANES
 
     def spread(step, carry):
@@ -692,11 +712,6 @@
     for c in range(4):
         mine[c : c + 1, :] = answer[c]
         mine[4 + c : 5 + c, :] = answer[c]
-    around = [
-        send(mine, others.at[sky], sc.at[number], rc.at[number], peer)
-        for number, peer in enumerate(peers)
-    ]
-    others[pl.ds(sky, 1)] = mine[...][None]
     reach = jnp.where(block < blocks - 1, span + 3, span)
     extended = jnp.where(lane < reach, mine[...], 0.0)
     windows = []
@@ -727,16 +742,33 @@
     lax.fori_loop(0, tiles // (SUB * unroll), last, 0)
     for copy in around:
         copy.wait_recv()
+    edges[0].wait_recv()
+    lane_all = lax.broadcasted_iota(jnp.int32, (owners, LANES), 1)
+    row_all = lax.broadcasted_iota(jnp.int32, (owners, LANES), 0)
+    entering = (lane_all < 3) & ((row_all > 0) | (time > 0))
+    wholes = []
+    for row in range(14):
+        head = pltpu.roll(gathered[pl.ds(row, owners, stride=16), :], LANES - span, 1)
+        wholes.append(gathered[pl.ds(16 + row, owners, stride=16), :] + jnp.where(entering, head, 0.0))
+    answer = damped_solve(wholes[:10], wholes[10:], 4, KNOT_PAIRS)
+    for c in range(4):
+        others[pl.ds(c, owners, stride=SUB), :] = answer[c]
     each = LANES // span
     for first in range(0, owners, each):
-        joined = jnp.where(lane < span, others[first], 0.0)
+        joined = jnp.where(lane < span, others[first * SUB : (first + 1) * SUB, :], 0.0)
         for number in range(1, each):
-            moved = pltpu.roll(others[first + number], number * span, 1)
+            block_at = (first + number) * SUB
+            moved = pltpu.roll(others[block_at : block_at + SUB, :], number * span, 1)
             keep = (lane >= number * span) & (lane < (number + 1) * span)
             joined = jnp.where(keep, moved, joined)
         knot_out[:, first * span : first * span + LANES] = joined[:4]
     for copy in pending:
         copy.wait_send()
+
+    @pl.when(last_of)
+    def _():
+        for copy in edges:
+            copy.wait_send()
 
 
 def settle(tile_pixel, pixel_slot, knots, residual, obs_weight, source_partials, attitude_partials, source_index, table, squares, span):
@@ -767,8 +799,9 @@
             pltpu.VMEM((16, LANES), f32),
             pltpu.VMEM(residual.shape, f32),
             pltpu.VMEM((tiles, 16), f32),
-            pltpu.VMEM((owners, SUB, LANES), f32),
-            dma, dma, dma, dma, dma, dma, dma((owners - 1,)), dma((owners - 1,)),
+            pltpu.VMEM((owners * SUB, LANES), f32),
+            pltpu.VMEM(((owners + 1) * 16, LANES), f32),
+            dma, dma, dma, dma, dma, dma, dma((owners - 1,)), dma((owners - 1,)), dma((owners,)), dma,
         ],
         compiler_params=pltpu.CompilerParams(
             collective_id=1, has_side_effects=True, vmem_limit_bytes=24 * MIB

time: 93.3 us -> 90.5 us (0.970)
  Pallas kernels: 92.2 us -> 89.5 us
    pallas_call x1, Pallas kernels: 67.9 us -> 65.6 us  [exchange(): pl.pallas_call(functools.partial(exchange_kernel, times, lines, subs, uni...]
where the time goes in v5:
time: 90.5 us; the launch traced here: 90.4 us
  Pallas kernels  89.5 us (99%)
    pallas_call x1, Pallas kernels, exchange(): pl.pallas_call(functools.partial(exchange_kernel, times, lines, subs, uni...  65.6 us
    pallas_call x1, Pallas kernels, settle(): pl.pallas_call(functools.partial(settle_kernel, times, owners, span), nam...  14.1 us
    pallas_call x1, Pallas kernels, local_sums(): pl.pallas_call(functools.partial(sums_kernel, tiles_step), name='local_su...  8.97 us

profile of v5, /device:TPU:0, one launch (start us, length us, event | category | flops | bytes accessed | tf_op | source)
XLA Modules:
  0.0 90.4 jit_solution(18049859244387187936)
XLA Ops:
  0.6 0.0 copy-start
  0.6 0.0 copy-start.2
  0.7 9.0 %local_sums.1 = f32[20480,128]{1,0:T(8,128)S(1)} custom-call(s32[512]{0:T(512)} %pixel_hbm.3, s32[1024]{0:T(1024)} %slot_hbm.3, f32[512,128]{1,0:T(8,128)} %resid.1, f32[512,128]{1,0:T(8,128)} %weight.3, f32[5,512,128]{2,1,0:T(8,128)} %parts.1, s32[512,128]{1,0:T(8,128)} %index.1), custom_call_target="tpu_custom_call" | custom-call | tf_op jit(solution)/shard_map/local_sums/pallas_call | solution.py:157
  9.6 0.0 copy-done
  9.6 0.0 copy-done.2
  9.6 0.0 copy-start.1
  9.7 0.0 copy-start.3
  9.7 0.0 copy-start.4
  9.7 0.0 copy-start.5
  9.7 0.0 copy-start.6
  9.7 0.0 copy-start.7
  9.7 65.6 %exchange.1 = (f32[5128,128]{1,0:T(8,128)S(1)}, f32[512,128]{1,0:T(8,128)S(1)}) custom-call(f32[4,2,4,640,128]{4,3,2,1,0:T(8,128)S(1)} %bitcast.2, f32[512,128]{1,0:T(8,128)S(1)} %copy-done.2, f32[16,512,128]{2,1,0:T(8,128)S(1)} %copy-done), custom_call_target="tpu_custom_call" | custom-call | tf_op jit(solution)/shard_map/exchange/pallas_call | solution.py:550
  75.3 0.0 copy-done.1
  75.4 0.0 copy-done.3
  75.4 0.0 copy-done.4
  75.4 0.0 copy-done.5
  75.4 0.0 copy-done.6
  75.4 0.0 copy-done.7
  75.4 14.1 %settle.1 = (f32[512,128]{1,0:T(8,128)S(1)}, f32[5,16384]{1,0:T(8,128)S(1)}, f32[4,512]{1,0:T(4,128)S(1)}) custom-call(s32[512]{0:T(512)S(1)} %copy-done.6, s32[1024]{0:T(1024)S(1)} %copy-done.5, s32[1,512]{1,0:T(1,128)S(1)} %bitcast.3, f32[512,128]{1,0:T(8,128)S(1)} %copy-done.3, f32[512,128]{1,0:T(8,128)S(1)} %copy-done.2, f32[5,512,128]{2,1,0:T(8,128)S(1)} %copy-done.1, ...), custom_call_target="tpu_custom_call" | custom-call | tf_op jit(solution)/shard_map/settle/pallas_call | solution.py:781
  89.5 0.9 %finish.1 = (f32[512,128]{1,0:T(8,128)}, f32[5,16384]{1,0:T(8,128)}, f32[4,512]{1,0:T(4,128)}) custom-call(f32[512,128]{1,0:T(8,128)S(1)} %get-tuple-element.10.refs_0_, f32[5,16384]{1,0:T(8,128)S(1)} %get-tuple-element.11.refs_1_, f32[4,512]{1,0:T(4,128)S(1)} %get-tuple-element.12.refs_2_), custom_call_target="tpu_custom_call" | custom-call | tf_op jit(solution)/shard_map/finish/pallas_call | solution.py:824
Async XLA Ops:
  0.6 9.0 %copy-start = (f32[16,512,128]{2,1,0:T(8,128)S(1)}, f32[16,512,128]{2,1,0:T(8,128)}, u32[]{:S(2)}) copy-start(f32[16,512,128]{2,1,0:T(8,128)} %att.3) | copy-start | bytes 12582916
  0.6 9.0 %copy-start.2 = (f32[512,128]{1,0:T(8,128)S(1)}, f32[512,128]{1,0:T(8,128)}, u32[]{:S(2)}) copy-start(f32[512,128]{1,0:T(8,128)} %weight.3) | copy-start | bytes 786436
  9.6 65.7 %copy-start.1 = (f32[5,512,128]{2,1,0:T(8,128)S(1)}, f32[5,512,128]{2,1,0:T(8,128)}, u32[]{:S(2)}) copy-start(f32[5,512,128]{2,1,0:T(8,128)} %parts.1) | copy-start | bytes 3932164
  9.7 65.7 %copy-start.3 = (f32[512,128]{1,0:T(8,128)S(1)}, f32[512,128]{1,0:T(8,128)}, u32[]{:S(2)}) copy-start(f32[512,128]{1,0:T(8,128)} %resid.1) | copy-start | bytes 786436
  9.7 65.7 %copy-start.4 = (s32[512,128]{1,0:T(8,128)S(1)}, s32[512,128]{1,0:T(8,128)}, u32[]{:S(2)}) copy-start(s32[512,128]{1,0:T(8,128)} %index.1) | copy-start | bytes 786436
  9.7 65.7 %copy-start.5 = (s32[1024]{0:T(1024)S(1)}, s32[1024]{0:T(1024)}, u32[]{:S(2)}) copy-start(s32[1024]{0:T(1024)} %slot_hbm.3) | copy-start | bytes 12292
  9.7 65.7 %copy-start.6 = (s32[512]{0:T(512)S(1)}, s32[512]{0:T(512)}, u32[]{:S(2)}) copy-start(s32[512]{0:T(512)} %pixel_hbm.3) | copy-start | bytes 6148
  9.7 65.7 %copy-start.7 = (s32[512]{0:T(512)S(1)}, s32[512]{0:T(512)}, u32[]{:S(2)}) copy-start(s32[512]{0:T(512)} %param.14) | copy-start | bytes 6148
